TPU v7x, 16 devices: a 4x2x1 block of a 4x4x8 slice. The times are simulated.
16 devices in a mesh: batch: 2 (over y, z), seq: 8 (over x, core).
Axes of the slice: x: 4, y: 2, z: 1, core: 2. Of those that a mesh axis runs over, the one named last changes fastest.
The devices are a block of a 4x4x8 slice.
Arguments:
- msa_act: bfloat16 [1024, 384, 64], P(('batch', 'seq')), parts along dimension 0
- msa_mask: int32 [1024, 384], P(('batch', 'seq')), parts along dimension 0
- pair_act: bfloat16 [768, 384, 128], P(('batch', 'seq')), parts along dimension 0
- w_pair_bias: bfloat16 [128, 8], replicated
- w_row_in: bfloat16 [64, 256], replicated
- b_row_gate: bfloat16 [64], replicated
- w_row_out: bfloat16 [64, 64], replicated
- w_col_in: bfloat16 [64, 144], replicated
- b_col_gate: bfloat16 [64], replicated
- w_col_out: bfloat16 [64, 64], replicated
- w_trans_in: bfloat16 [64, 256], replicated
- w_trans_out: bfloat16 [256, 64], replicated
- w_opm_in: bfloat16 [64, 64], replicated
- w_opm_out: bfloat16 [32, 32, 128], replicated
- b_opm_out: bfloat16 [128], replicated
Outputs:
- output 1: bfloat16 [1024, 384, 64], P(('batch', 'seq')), parts along dimension 0
- output 2: bfloat16 [768, 384, 128], P(('batch', 'seq')), parts along dimension 0
There are 2 independent parts. A program takes and returns all parts, laid end to end along the dimension named above; an argument that names none is the same for every part.
All inputs are finite; a program needn't handle non-finite values.
Results may differ from a plain program's by a relative error of at most 0.0113807.
Values are sent between devices in bfloat16 or wider.
A program may use at most 768 MiB of HBM per device.

v0:
```python
import jax
import jax.numpy as jnp
from jax import lax
from jax.sharding import PartitionSpec as P, NamedSharding

MASK_FILL = -1e9


def layer_norm(values):
    as_float = values.astype(jnp.float32)
    centered = as_float - jnp.mean(as_float, axis=-1, keepdims=True)
    variance = jnp.mean(centered * centered, axis=-1, keepdims=True)
    return (centered * lax.rsqrt(variance + 1e-5)).astype(jnp.bfloat16)


def solution(mesh):
    row_spec = P(('batch', 'seq'))
    rep_spec = P()

    def local_block(value_a7, value_a8, pair_act, w_pair_bias, w_row_in, b_row_gate, w_row_out, w_col_in, b_col_gate, w_col_out, w_trans_in, w_trans_out, w_opm_in, w_opm_out, b_opm_out):
        seq_local, num_res, array_b7 = value_a7.shape
        pair_dim = pair_act.shape[-1]
        num_heads = w_pair_bias.shape[1]
        head_total = w_row_out.shape[0]
        head_dim = head_total // num_heads
        opm_dim = w_opm_out.shape[0]
        attn_scale = head_dim ** -0.5
        seq_blk = 4
        row_blk = 16
        keep_mask = value_a8 > 0
        mask_bf = value_a8.astype(jnp.bfloat16)

        bias_rows = jnp.einsum('ijc,ch->hij', layer_norm(pair_act), w_pair_bias, preferred_element_type=jnp.float32).astype(jnp.bfloat16)
        pair_bias = lax.all_gather(bias_rows, 'seq', axis=1, tiled=True)

        row_proj = jnp.einsum('sic,cghd->gsihd', layer_norm(value_a7), w_row_in.reshape(array_b7, 4, num_heads, head_dim), preferred_element_type=jnp.float32).astype(jnp.bfloat16)
        row_proj = row_proj.reshape(4, seq_local // seq_blk, seq_blk, num_res, num_heads, head_dim)
        mask_blocks = keep_mask.reshape(seq_local // seq_blk, seq_blk, num_res)
        gate_bias = b_row_gate.astype(jnp.float32).reshape(num_heads, head_dim)

        def attend_block(block_in):
            q_blk, k_blk, v_blk, g_blk, m_blk = block_in
            scores = jnp.einsum('sihd,sjhd->shij', q_blk, k_blk, preferred_element_type=jnp.float32) * attn_scale + pair_bias
            scores = jnp.where(m_blk[:, None, None, :], scores, MASK_FILL)
            attn_probs = jax.nn.softmax(scores, axis=-1).astype(jnp.bfloat16)
            attended = jnp.einsum('shij,sjhd->sihd', attn_probs, v_blk, preferred_element_type=jnp.float32)
            return (jax.nn.sigmoid(g_blk.astype(jnp.float32) + gate_bias) * attended).astype(jnp.bfloat16)

        gated_row = lax.map(attend_block, (row_proj[0], row_proj[1], row_proj[2], row_proj[3], mask_blocks))
        gated_row = gated_row.reshape(seq_local, num_res, head_total)
        local_c7 = (value_a7 + jnp.einsum('sif,fc->sic', gated_row, w_row_out, preferred_element_type=jnp.float32)).astype(jnp.bfloat16)

        col_proj = jnp.einsum('sic,cf->sif', layer_norm(local_c7), w_col_in, preferred_element_type=jnp.float32).astype(jnp.bfloat16)
        q_col = col_proj[:, :, :head_total].reshape(seq_local, num_res, num_heads, head_dim)
        g_col = col_proj[:, :, head_total:2 * head_total]
        k_col = col_proj[:, :, 2 * head_total:2 * head_total + head_dim]
        v_col = col_proj[:, :, 2 * head_total + head_dim:]
        q_sum = jnp.einsum('si,sihd->ihd', mask_bf, q_col, preferred_element_type=jnp.float32)
        counts = jnp.sum(value_a8, axis=0).astype(jnp.float32)
        q_sum, counts = lax.psum((q_sum, counts), 'seq')
        q_bar = (q_sum / (counts[:, None, None] + 1e-10)).astype(jnp.bfloat16)
        logits = jnp.einsum('ihd,sid->sih', q_bar, k_col, preferred_element_type=jnp.float32) * attn_scale
        logits = jnp.where(keep_mask[:, :, None], logits, MASK_FILL)
        local_max = jnp.max(logits, axis=0)
        weights = jnp.exp(logits - local_max)
        local_den = jnp.sum(weights, axis=0)
        local_num = jnp.einsum('sih,sid->ihd', weights, v_col, preferred_element_type=jnp.float32)
        global_max = lax.pmax(local_max, 'seq')
        rescale = jnp.exp(local_max - global_max)
        total_den, total_num = lax.psum((local_den * rescale, local_num * rescale[:, :, None]), 'seq')
        col_out = (total_num / total_den[:, :, None]).reshape(num_res, head_total)
        col_gate = jax.nn.sigmoid(g_col.astype(jnp.float32) + b_col_gate.astype(jnp.float32))
        gated_col = (col_gate * col_out).astype(jnp.bfloat16)
        piece_d7 = (local_c7 + jnp.einsum('sif,fc->sic', gated_col, w_col_out, preferred_element_type=jnp.float32)).astype(jnp.bfloat16)

        hidden = jnp.maximum(jnp.einsum('sic,cf->sif', layer_norm(piece_d7), w_trans_in, preferred_element_type=jnp.float32), 0.0).astype(jnp.bfloat16)
        value_a9 = (piece_d7 + jnp.einsum('sif,fc->sic', hidden, w_trans_out, preferred_element_type=jnp.float32)).astype(jnp.bfloat16)

        opm_proj = jnp.einsum('sic,cf->sif', layer_norm(value_a9), w_opm_in, preferred_element_type=jnp.float32).astype(jnp.bfloat16) * mask_bf[:, :, None]
        left_vec = opm_proj[:, :, :opm_dim]
        right_vec = opm_proj[:, :, opm_dim:]
        left_blocks = jnp.moveaxis(left_vec.reshape(seq_local, num_res // row_blk, row_blk, opm_dim), 1, 0)
        w_opm_float = w_opm_out.astype(jnp.float32)

        def outer_block(left_blk):
            outer_sum = jnp.einsum('sic,sjd->ijcd', left_blk, right_vec, preferred_element_type=jnp.float32)
            return jnp.einsum('ijcd,cde->ije', outer_sum, w_opm_float)

        local_pair = lax.map(outer_block, left_blocks).reshape(num_res, num_res, pair_dim)
        norm_part = jnp.einsum('si,sj->ij', mask_bf, mask_bf, preferred_element_type=jnp.float32)
        pair_sum = lax.psum_scatter(local_pair, 'seq', scatter_dimension=0, tiled=True)
        norm_sum = lax.psum_scatter(norm_part, 'seq', scatter_dimension=0, tiled=True)
        pair_out = (pair_act + pair_sum / (norm_sum[:, :, None] + 1e-3) + b_opm_out).astype(jnp.bfloat16)
        return value_a9, pair_out

    return jax.shard_map(local_block, mesh=mesh, in_specs=(row_spec, row_spec, row_spec) + (rep_spec,) * 12, out_specs=(row_spec, row_spec), check_vma=False)
```

profile of v0, /device:TPU:113, one launch (start us, length us, event | category | flops | bytes accessed | tf_op | source)
XLA Modules:
  0.0 1271.3 jit_solution(3188441517306200391)
XLA Ops:
  27.1 14.6 %psum.29 = f32[384]{0:T(512)S(1)} all-reduce(f32[384]{0:T(512)S(1)} %convert_element_type.129), channel_id=1, replica_groups=mesh['batch'=2,'seq'=8] {'seq'}, use_global_device_ids=true, to_apply=%region_12.13 | all-reduce | flops 384 | bytes 3072 | tf_op jit(solution)/shard_map/psum | solution.py:60
  63.2 405.6 %while.20 = (s32[]{:T(128)}, bf16[16,4,384,8,8]{2,4,3,1,0:T(8,128)(2,1)}, bf16[16,4,384,8,8]{2,4,3,1,0:T(8,128)(2,1)}, f32[64]{0:T(128)S(1)}, bf16[16,4,384,8,8]...) while((s32[]{:T(128)}, ...), condition=%wide.region_7.8_spmd, body=%wide.region_4.7_spmd.sunk | while | flops 185893248 | bytes 50634088 | solution.py:49
  65.7 14.2 %fusion.176 = (f32[4,8,384]{2,1,0:T(8,128)S(1)}, f32[4,8,384,384]{2,3,1,0:T(8,128)}) fusion(f32[8,384,384]{1,2,0:T(8,128)} %convert_element_type.304, pred[4,384]{1,0:T(4,128)(4,1)S(1)} %dynamic-slice_bitcast_fusion.2, bf16[16,4,384,8,8]{2,4,3,1,0:T(8,128)(2,1)} %get-tuple-element.288, s32[]{:T(128)} %get-tuple-element.271, ...), kind=kOutput, calls=%fused_computation.149.clone.1 | convolution fusion | flops 99090816 | bytes 24037888 | tf_op jit(solution)/shard_map/while/body/eval_jaxpr/sub | solution.py:45
  91.1 14.2 %fusion.176 = (f32[4,8,384]{2,1,0:T(8,128)S(1)}, f32[4,8,384,384]{2,3,1,0:T(8,128)}) fusion(f32[8,384,384]{1,2,0:T(8,128)} %convert_element_type.304, pred[4,384]{1,0:T(4,128)(4,1)S(1)} %dynamic-slice_bitcast_fusion.2, bf16[16,4,384,8,8]{2,4,3,1,0:T(8,128)(2,1)} %get-tuple-element.288, s32[]{:T(128)} %get-tuple-element.271, ...), kind=kOutput, calls=%fused_computation.149.clone.1 | convolution fusion | flops 99090816 | bytes 24037888 | tf_op jit(solution)/shard_map/while/body/eval_jaxpr/sub | solution.py:45
  116.4 14.2 %fusion.176 = (f32[4,8,384]{2,1,0:T(8,128)S(1)}, f32[4,8,384,384]{2,3,1,0:T(8,128)}) fusion(f32[8,384,384]{1,2,0:T(8,128)} %convert_element_type.304, pred[4,384]{1,0:T(4,128)(4,1)S(1)} %dynamic-slice_bitcast_fusion.2, bf16[16,4,384,8,8]{2,4,3,1,0:T(8,128)(2,1)} %get-tuple-element.288, s32[]{:T(128)} %get-tuple-element.271, ...), kind=kOutput, calls=%fused_computation.149.clone.1 | convolution fusion | flops 99090816 | bytes 24037888 | tf_op jit(solution)/shard_map/while/body/eval_jaxpr/sub | solution.py:45
  141.7 14.2 %fusion.176 = (f32[4,8,384]{2,1,0:T(8,128)S(1)}, f32[4,8,384,384]{2,3,1,0:T(8,128)}) fusion(f32[8,384,384]{1,2,0:T(8,128)} %convert_element_type.304, pred[4,384]{1,0:T(4,128)(4,1)S(1)} %dynamic-slice_bitcast_fusion.2, bf16[16,4,384,8,8]{2,4,3,1,0:T(8,128)(2,1)} %get-tuple-element.288, s32[]{:T(128)} %get-tuple-element.271, ...), kind=kOutput, calls=%fused_computation.149.clone.1 | convolution fusion | flops 99090816 | bytes 24037888 | tf_op jit(solution)/shard_map/while/body/eval_jaxpr/sub | solution.py:45
  167.1 14.2 %fusion.176 = (f32[4,8,384]{2,1,0:T(8,128)S(1)}, f32[4,8,384,384]{2,3,1,0:T(8,128)}) fusion(f32[8,384,384]{1,2,0:T(8,128)} %convert_element_type.304, pred[4,384]{1,0:T(4,128)(4,1)S(1)} %dynamic-slice_bitcast_fusion.2, bf16[16,4,384,8,8]{2,4,3,1,0:T(8,128)(2,1)} %get-tuple-element.288, s32[]{:T(128)} %get-tuple-element.271, ...), kind=kOutput, calls=%fused_computation.149.clone.1 | convolution fusion | flops 99090816 | bytes 24037888 | tf_op jit(solution)/shard_map/while/body/eval_jaxpr/sub | solution.py:45
  192.4 14.2 %fusion.176 = (f32[4,8,384]{2,1,0:T(8,128)S(1)}, f32[4,8,384,384]{2,3,1,0:T(8,128)}) fusion(f32[8,384,384]{1,2,0:T(8,128)} %convert_element_type.304, pred[4,384]{1,0:T(4,128)(4,1)S(1)} %dynamic-slice_bitcast_fusion.2, bf16[16,4,384,8,8]{2,4,3,1,0:T(8,128)(2,1)} %get-tuple-element.288, s32[]{:T(128)} %get-tuple-element.271, ...), kind=kOutput, calls=%fused_computation.149.clone.1 | convolution fusion | flops 99090816 | bytes 24037888 | tf_op jit(solution)/shard_map/while/body/eval_jaxpr/sub | solution.py:45
  217.8 14.2 %fusion.176 = (f32[4,8,384]{2,1,0:T(8,128)S(1)}, f32[4,8,384,384]{2,3,1,0:T(8,128)}) fusion(f32[8,384,384]{1,2,0:T(8,128)} %convert_element_type.304, pred[4,384]{1,0:T(4,128)(4,1)S(1)} %dynamic-slice_bitcast_fusion.2, bf16[16,4,384,8,8]{2,4,3,1,0:T(8,128)(2,1)} %get-tuple-element.288, s32[]{:T(128)} %get-tuple-element.271, ...), kind=kOutput, calls=%fused_computation.149.clone.1 | convolution fusion | flops 99090816 | bytes 24037888 | tf_op jit(solution)/shard_map/while/body/eval_jaxpr/sub | solution.py:45
  243.1 14.2 %fusion.176 = (f32[4,8,384]{2,1,0:T(8,128)S(1)}, f32[4,8,384,384]{2,3,1,0:T(8,128)}) fusion(f32[8,384,384]{1,2,0:T(8,128)} %convert_element_type.304, pred[4,384]{1,0:T(4,128)(4,1)S(1)} %dynamic-slice_bitcast_fusion.2, bf16[16,4,384,8,8]{2,4,3,1,0:T(8,128)(2,1)} %get-tuple-element.288, s32[]{:T(128)} %get-tuple-element.271, ...), kind=kOutput, calls=%fused_computation.149.clone.1 | convolution fusion | flops 99090816 | bytes 24037888 | tf_op jit(solution)/shard_map/while/body/eval_jaxpr/sub | solution.py:45
  268.4 14.2 %fusion.176 = (f32[4,8,384]{2,1,0:T(8,128)S(1)}, f32[4,8,384,384]{2,3,1,0:T(8,128)}) fusion(f32[8,384,384]{1,2,0:T(8,128)} %convert_element_type.304, pred[4,384]{1,0:T(4,128)(4,1)S(1)} %dynamic-slice_bitcast_fusion.2, bf16[16,4,384,8,8]{2,4,3,1,0:T(8,128)(2,1)} %get-tuple-element.288, s32[]{:T(128)} %get-tuple-element.271, ...), kind=kOutput, calls=%fused_computation.149.clone.1 | convolution fusion | flops 99090816 | bytes 24037888 | tf_op jit(solution)/shard_map/while/body/eval_jaxpr/sub | solution.py:45
  293.8 14.2 %fusion.176 = (f32[4,8,384]{2,1,0:T(8,128)S(1)}, f32[4,8,384,384]{2,3,1,0:T(8,128)}) fusion(f32[8,384,384]{1,2,0:T(8,128)} %convert_element_type.304, pred[4,384]{1,0:T(4,128)(4,1)S(1)} %dynamic-slice_bitcast_fusion.2, bf16[16,4,384,8,8]{2,4,3,1,0:T(8,128)(2,1)} %get-tuple-element.288, s32[]{:T(128)} %get-tuple-element.271, ...), kind=kOutput, calls=%fused_computation.149.clone.1 | convolution fusion | flops 99090816 | bytes 24037888 | tf_op jit(solution)/shard_map/while/body/eval_jaxpr/sub | solution.py:45
  319.1 14.2 %fusion.176 = (f32[4,8,384]{2,1,0:T(8,128)S(1)}, f32[4,8,384,384]{2,3,1,0:T(8,128)}) fusion(f32[8,384,384]{1,2,0:T(8,128)} %convert_element_type.304, pred[4,384]{1,0:T(4,128)(4,1)S(1)} %dynamic-slice_bitcast_fusion.2, bf16[16,4,384,8,8]{2,4,3,1,0:T(8,128)(2,1)} %get-tuple-element.288, s32[]{:T(128)} %get-tuple-element.271, ...), kind=kOutput, calls=%fused_computation.149.clone.1 | convolution fusion | flops 99090816 | bytes 24037888 | tf_op jit(solution)/shard_map/while/body/eval_jaxpr/sub | solution.py:45
  344.5 14.2 %fusion.176 = (f32[4,8,384]{2,1,0:T(8,128)S(1)}, f32[4,8,384,384]{2,3,1,0:T(8,128)}) fusion(f32[8,384,384]{1,2,0:T(8,128)} %convert_element_type.304, pred[4,384]{1,0:T(4,128)(4,1)S(1)} %dynamic-slice_bitcast_fusion.2, bf16[16,4,384,8,8]{2,4,3,1,0:T(8,128)(2,1)} %get-tuple-element.288, s32[]{:T(128)} %get-tuple-element.271, ...), kind=kOutput, calls=%fused_computation.149.clone.1 | convolution fusion | flops 99090816 | bytes 24037888 | tf_op jit(solution)/shard_map/while/body/eval_jaxpr/sub | solution.py:45
  395.1 14.2 %fusion.176 = (f32[4,8,384]{2,1,0:T(8,128)S(1)}, f32[4,8,384,384]{2,3,1,0:T(8,128)}) fusion(f32[8,384,384]{1,2,0:T(8,128)} %convert_element_type.304, pred[4,384]{1,0:T(4,128)(4,1)S(1)} %dynamic-slice_bitcast_fusion.2, bf16[16,4,384,8,8]{2,4,3,1,0:T(8,128)(2,1)} %get-tuple-element.288, s32[]{:T(128)} %get-tuple-element.271, ...), kind=kOutput, calls=%fused_computation.149.clone.1 | convolution fusion | flops 99090816 | bytes 24037888 | tf_op jit(solution)/shard_map/while/body/eval_jaxpr/sub | solution.py:45
  420.5 14.2 %fusion.176 = (f32[4,8,384]{2,1,0:T(8,128)S(1)}, f32[4,8,384,384]{2,3,1,0:T(8,128)}) fusion(f32[8,384,384]{1,2,0:T(8,128)} %convert_element_type.304, pred[4,384]{1,0:T(4,128)(4,1)S(1)} %dynamic-slice_bitcast_fusion.2, bf16[16,4,384,8,8]{2,4,3,1,0:T(8,128)(2,1)} %get-tuple-element.288, s32[]{:T(128)} %get-tuple-element.271, ...), kind=kOutput, calls=%fused_computation.149.clone.1 | convolution fusion | flops 99090816 | bytes 24037888 | tf_op jit(solution)/shard_map/while/body/eval_jaxpr/sub | solution.py:45
  445.8 14.2 %fusion.176 = (f32[4,8,384]{2,1,0:T(8,128)S(1)}, f32[4,8,384,384]{2,3,1,0:T(8,128)}) fusion(f32[8,384,384]{1,2,0:T(8,128)} %convert_element_type.304, pred[4,384]{1,0:T(4,128)(4,1)S(1)} %dynamic-slice_bitcast_fusion.2, bf16[16,4,384,8,8]{2,4,3,1,0:T(8,128)(2,1)} %get-tuple-element.288, s32[]{:T(128)} %get-tuple-element.271, ...), kind=kOutput, calls=%fused_computation.149.clone.1 | convolution fusion | flops 99090816 | bytes 24037888 | tf_op jit(solution)/shard_map/while/body/eval_jaxpr/sub | solution.py:45
  488.9 48.2 %all-reduce.3.cloned.1.call-done = f32[384,8,8]{2,1,0:T(8,128)} async-done(((f32[384,8,8]{2,1,0:T(8,128)}), f32[384,8,8]{2,1,0:T(8,128)}) %all-reduce.3.cloned.1.call-update) | async-done | bytes 98320 | tf_op jit(solution)/shard_map/psum | solution.py:60
  540.6 26.2 %pmax.7 = f32[384,8]{1,0:T(8,128)} all-reduce(f32[384,8]{1,0:T(8,128)S(1)} %get-tuple-element.165), channel_id=1, replica_groups=mesh['batch'=2,'seq'=8] {'seq'}, use_global_device_ids=true, to_apply=%region_14.15 | all-reduce | flops 3072 | bytes 24576 | tf_op jit(solution)/shard_map/pmax | solution.py:68
  575.9 28.3 %psum.31 = f32[384,8]{1,0:T(8,128)S(1)} all-reduce(f32[384,8]{1,0:T(8,128)} %get-tuple-element.148), channel_id=1, replica_groups=mesh['batch'=2,'seq'=8] {'seq'}, use_global_device_ids=true, to_apply=%region_17.18 | all-reduce | flops 3072 | bytes 24576 | tf_op jit(solution)/shard_map/psum | solution.py:70
  604.2 26.4 %all-reduce.5.cloned.1.call-done = f32[384,8,8]{2,1,0:T(8,128)} async-done(((f32[384,8,8]{2,1,0:T(8,128)}), f32[384,8,8]{2,1,0:T(8,128)}) %all-reduce.5.cloned.1.call-update) | async-done | bytes 98320 | tf_op jit(solution)/shard_map/psum | solution.py:70
  642.2 14.9 %convert_reduce_fusion.4 = (f32[64,384]{1,0:T(8,128)S(1)}, bf16[64,384,64]{1,2,0:T(8,128)(2,1)S(1)}) fusion(bf16[256,64]{0,1:T(8,128)(2,1)S(1)} %copy-done.14, bf16[64,384,64]{1,2,0:T(8,128)(2,1)} %copy-done.5, f32[64,384]{1,0:T(8,128)S(1)} %add_rsqrt_fusion.1, f32[64,384]{1,0:T(8,128)S(1)} %broadcast_multiply_fusion.1, bf16[64,256]{1,0:T(8,128)(2,1)} %param.29), kind=kOutput, calls=%fused_computation.71 | convolution fusion | flops 1637326848 | bytes 6651904 | tf_op jit(solution)/shard_map/sif,fc->sic/dot_general | solution.py:77
  668.0 223.6 %while.21 = (s32[]{:T(128)}, f32[24,16,384,128]{3,2,1,0:T(8,128)}, bf16[24,64,16,32]{1,3,2,0:T(8,128)(2,1)}, bf16[64,384,32]{1,0,2:T(8,128)(2,1)S(1)}, bf16[32,32,128]{2,1,0:T(8,128)(2,1)S(1)}, /*index=5*/s32[]{:T(128)}) while((s32[]{:T(128)}, f32[24,16,384,128]{3,2,1,0:T(8,128)}, bf16[24,64,16,32]{1,3,2,0:T(8,128)(2,1)}, ...), condition=%wide.region_23.24_spmd, body=%wide.region_22.23_spmd.sunk | while | flops 2415919104 | bytes 5112901 | solution.py:89
  893.2 362.7 %reduce-scatter.3.cloned.1.call-done = f32[48,384,128]{2,1,0:T(8,128)} async-done(((f32[384,384,128]{2,1,0:T(8,128)}), f32[48,384,128]{2,1,0:T(8,128)}) %reduce-scatter.3.cloned.1.call-update) | async-done | bytes 9437200 | tf_op jit(solution)/shard_map/reduce_scatter | solution.py:91
  (195 shorter events, 521.9 us)
Async XLA Ops:
  7.2 467.0 %copy-start = (bf16[64,144]{1,0:T(8,128)(2,1)S(1)}, bf16[64,144]{1,0:T(8,128)(2,1)}, u32[]{:S(2)}) copy-start(bf16[64,144]{1,0:T(8,128)(2,1)} %param.26) | copy-start | bytes 55300
  7.2 9.5 copy-start.16
  7.2 52.7 %all-gather.2.cloned.1.call-start = ((), (), s32[]{:S(2)}) async-start(), calls=%async_computation.2 | async-start | bytes 2654208 | tf_op jit(solution)/shard_map/all_gather | solution.py:34
  7.3 3.8 copy-start.2
  16.6 8.8 copy-start.8
  16.6 9.7 copy-start.10
  16.6 9.8 copy-start.17
  16.7 25.6 %copy-start.1 = (bf16[64,384,64]{1,2,0:T(8,128)(2,1)S(1)}, bf16[64,384,64]{1,2,0:T(8,128)(2,1)}, u32[]{:S(2)}) copy-start(bf16[64,384,64]{1,2,0:T(8,128)(2,1)} %param.19) | copy-start | bytes 9437188
  25.4 511.7 %all-reduce.3.cloned.1.call-start = ((), (), s32[]{:S(2)}) async-start(), calls=%async_computation.3 | async-start | bytes 3145728 | tf_op jit(solution)/shard_map/psum | solution.py:60
  63.2 405.6 %copy-start.11 = (bf16[64,64]{1,0:T(8,128)(2,1)S(1)}, bf16[64,64]{1,0:T(8,128)(2,1)}, u32[]{:S(2)}) copy-start(bf16[64,64]{1,0:T(8,128)(2,1)} %param.25) | copy-start | bytes 24580
  474.2 5.1 copy-start.7
  476.3 3.0 copy-start.3
  479.3 57.8 %copy-start.9 = (pred[64,384]{0,1:T(8,128)(4,1)S(1)}, pred[64,384]{0,1:T(8,128)(4,1)}, u32[]{:S(2)}) copy-start(pred[64,384]{0,1:T(8,128)(4,1)} %copy.47) | copy-start | bytes 73732
  479.3 57.8 %copy-start.12 = (f32[384]{0:T(512)S(1)}, f32[384]{0:T(512)}, u32[]{:S(2)}) copy-start(f32[384]{0:T(512)} %broadcast_add_fusion.1) | copy-start | bytes 4612
  481.8 148.8 %all-reduce.5.cloned.1.call-start = ((), (), s32[]{:S(2)}) async-start(), calls=%async_computation.4 | async-start | bytes 3145728 | tf_op jit(solution)/shard_map/psum | solution.py:70
  569.1 5.5 copy-start.6
  569.1 6.7 copy-start.18
  574.5 61.0 %copy-start.15 = (bf16[64,64]{1,0:T(8,128)(2,1)S(1)}, bf16[64,64]{1,0:T(8,128)(2,1)}, u32[]{:S(2)}) copy-start(bf16[64,64]{1,0:T(8,128)(2,1)} %param.28) | copy-start | bytes 24580
  574.5 317.7 %reduce-scatter.5.cloned.1.call-start = ((), (), s32[]{:S(2)}) async-start(), calls=%async_computation.6 | async-start | bytes 663552 | tf_op jit(solution)/shard_map/reduce_scatter | solution.py:92
  575.8 680.0 %reduce-scatter.3.cloned.1.call-start = ((), (), s32[]{:S(2)}) async-start(), calls=%async_computation.5 | async-start | bytes 84934656 | tf_op jit(solution)/shard_map/reduce_scatter | solution.py:91
  635.5 6.7 copy-start.14
  640.5 1.7 copy-start.5
  657.1 1.7 copy-start.4
  661.3 6.7 copy-start.13
  (1 other events, 0.7 us)
Sparse Core Ops, SparseCore 0:
  25.5 24.9 all-gather.1
  481.9 55.1 all-reduce.2
  574.7 55.8 all-reduce.4
  632.7 25.9 reduce-scatter.4
  891.8 364.0 reduce-scatter.2
where the time goes:
time: 1280 us; the launch traced here: 1270 us
  matrix products  639 us (50%)
  waiting for transfers between devices  438 us (34%)
  other arithmetic  73.9 us (6%)
  blocking collectives  69.1 us (5%)
  local copies, waits for them, and re-layouts  36.3 us (3%)
  between operations  14.7 us (1%)
    reduce_scatter x1, waiting for transfers between devices, local_block(): lax.psum_scatter(local_pair, 'seq', scatter_dimension=0, tiled=True)  363 us
    sub x16, matrix products, attend_block(): attn_probs = jax.nn.softmax(scores, axis=-1).astype(jnp.bfloat16)  227 us
    dot_general x24, matrix products, outer_block(): return jnp.einsum('ijcd,cde->ije', outer_sum, w_opm_float)  224 us
    dot_general x16, matrix products, attend_block(): jnp.einsum('shij,sjhd->sihd', attn_probs, v_blk, preferred_element_type=j...  137 us
    psum x1, waiting for transfers between devices, local_block(): q_sum, counts = lax.psum((q_sum, counts), 'seq')  48.2 us
    convert_element_type x16, other arithmetic, attend_block(): jnp.einsum('sihd,sjhd->shij', q_blk, k_blk, preferred_element_type=jnp.fl...  40.1 us
    psum x1, blocking collectives, local_block(): lax.psum((local_den * rescale, local_num * rescale[:, :, None]), 'seq')  28.3 us
    psum x1, waiting for transfers between devices, local_block(): lax.psum((local_den * rescale, local_num * rescale[:, :, None]), 'seq')  26.4 us
  transfers between devices with their start and end apart: 5, of which 3 were waited for; matrix products, arithmetic and copies ran while one was open for 23% of the time, Pallas kernels for 0%

commit v1 on v0

v1 whole, which is shorter than its diff:
```python
import functools
import math

import jax
import jax.numpy as jnp
from jax import lax
from jax.experimental import pallas as pl
from jax.experimental.pallas import tpu as pltpu
from jax.sharding import PartitionSpec as P

MASK_FILL = -1e9
LOG2E = math.log2(math.e)
F32 = jnp.float32
BF16 = jnp.bfloat16
VMEM_LIMIT = 62 * 1024 * 1024
MESH = pl.DeviceIdType.MESH
SEQS = 4


def layer_norm(values):
    as_float = values.astype(F32)
    centered = as_float - jnp.mean(as_float, axis=-1, keepdims=True)
    variance = jnp.mean(centered * centered, axis=-1, keepdims=True)
    return (centered * lax.rsqrt(variance + 1e-5)).astype(BF16)


def norm_rows(x):
    c = x - jnp.mean(x, axis=0, keepdims=True)
    var = jnp.mean(c * c, axis=0, keepdims=True)
    return (c * lax.rsqrt(var + 1e-5)).astype(BF16)


def dot(a, b):
    return jnp.dot(a, b, preferred_element_type=F32)


def dot_t(a, b):
    return lax.dot_general(a, b, (((1,), (1,)), ((), ())), preferred_element_type=F32)


def sigmoid(x):
    return 1.0 / (1.0 + jnp.exp(-x))


def wide_max(x):
    return jnp.max(jnp.max(x, axis=0, keepdims=True), axis=1, keepdims=True)[0, 0]


def row_kernel(heads, hd, scale, e_ref, m_ref, bias_ref, win_ref, bg_ref, wout_ref, cin_ref,
               e1_ref, g_ref, kv_ref, qsum_ref, rhs_ref, kaug_ref, va_ref, att_ref, top_ref):
    us, res, ch = e_ref.shape
    ht = heads * hd
    wide = us * res
    step = pl.program_id(0)

    @pl.when(step == 0)
    def _():
        rows = lax.broadcasted_iota(jnp.int32, rhs_ref.shape, 1)
        rhs_ref[...] = jnp.where(rows == 2 * ht, 1.0, 0.0).astype(BF16)
        qsum_ref[...] = jnp.zeros_like(qsum_ref)
        top = jnp.abs(bias_ref[0])
        for pr in range(1, heads // 2):
            top = jnp.maximum(top, jnp.abs(bias_ref[pr]))
        top_ref[0] = wide_max(top)

    eye = (lax.broadcasted_iota(jnp.int32, (ch, ch), 0) == lax.broadcasted_iota(jnp.int32, (ch, ch), 1)).astype(BF16)
    x = dot_t(eye, e_ref[...].reshape(wide, ch))
    proj = dot(win_ref[...], norm_rows(x)).astype(BF16).astype(F32)
    q, k, v, g = (proj[n * ht:(n + 1) * ht] for n in range(4))
    keep = m_ref[0]
    qs = q * (scale * LOG2E)
    q_top = wide_max(jnp.sum((qs * qs).reshape(heads, hd, wide), axis=1))
    k_top = wide_max(jnp.sum((k * k).reshape(heads, hd, wide), axis=1))
    small = (q_top * k_top < 900.0) & (top_ref[0] < 30.0)

    first_half = (lax.broadcasted_iota(jnp.int32, (ht, wide), 0) % 16) < 8
    hi = qs.astype(BF16).astype(F32)
    for n, part in enumerate((hi, qs - hi)):
        even = jnp.where(first_half, part, 0.0).astype(BF16)
        odd = jnp.where(first_half, 0.0, part).astype(BF16)
        for u in range(us):
            for h in range(heads):
                rows = slice(16 * (h // 2), 16 * (h // 2) + 16)
                rhs_ref[u, n * ht + rows.start:n * ht + rows.stop, h * res:(h + 1) * res] = \
                    (odd if h % 2 else even)[rows, u * res:(u + 1) * res]
    pen = jnp.where(lax.broadcasted_iota(jnp.int32, (16, wide), 0) == 0,
                    jnp.broadcast_to(jnp.where(keep > 0, 0.0, -1e30), (16, wide)), 0.0)
    kaug_ref[...] = jnp.transpose(jnp.concatenate([k, k, pen], axis=0)).astype(BF16)
    ones = jnp.where(lax.broadcasted_iota(jnp.int32, (8, wide), 0) == 0, 1.0, 0.0)
    for pr in range(heads // 2):
        va_ref[pr] = jnp.concatenate([v[16 * pr:16 * pr + 8], ones, v[16 * pr + 8:16 * pr + 16], ones], axis=0).astype(BF16)

    @pl.when(small)
    def _():
        for u in range(us):
            cols = slice(u * res, (u + 1) * res)
            for pr in range(heads // 2):
                s = dot(kaug_ref[cols], rhs_ref[u, :, 2 * pr * res:(2 * pr + 2) * res]) + bias_ref[pr]
                o = dot(va_ref[pr, :, cols], jnp.exp2(s).astype(BF16))
                att_ref[16 * pr:16 * pr + 8, cols] = o[0:8, :res] / o[8:9, :res]
                att_ref[16 * pr + 8:16 * pr + 16, cols] = o[16:24, res:] / o[24:25, res:]
            some = jnp.max(keep[:, cols], axis=1, keepdims=True) > 0
            flat = jnp.mean(v[:, cols], axis=1, keepdims=True)
            att_ref[:, cols] = jnp.where(some, att_ref[:, cols], flat)

    @pl.when(jnp.logical_not(small))
    def _():
        def one(t, _):
            u, pr = t // (heads // 2), t % (heads // 2)
            cols = pl.ds(pl.multiple_of(u * res, res), res)
            s = dot(kaug_ref[cols], rhs_ref[u, :, pl.ds(pl.multiple_of(2 * pr * res, 2 * res), 2 * res)]) + bias_ref[pr]
            p = jnp.exp2(s - jnp.max(s, axis=0, keepdims=True)).astype(BF16)
            o = dot(va_ref[pr, :, cols], p)
            att_ref[pl.ds(pl.multiple_of(16 * pr, 16), 8), cols] = o[0:8, :res] / o[8:9, :res]
            att_ref[pl.ds(pl.multiple_of(16 * pr + 8, 8), 8), cols] = o[16:24, res:] / o[24:25, res:]
            return 0

        lax.fori_loop(0, us * (heads // 2), one, 0)

    gated = (sigmoid(g + bg_ref[...]) * att_ref[...]).astype(BF16)
    e1 = (x + dot(wout_ref[...], gated)).astype(BF16)
    e1_ref[0] = e1
    col = dot(cin_ref[...], norm_rows(e1.astype(F32))).astype(BF16)
    part = col[:ht].astype(F32) * keep
    tot = part[:, :res]
    for u in range(1, us):
        tot = tot + part[:, u * res:(u + 1) * res]
    qsum_ref[...] += tot
    g_ref[0] = col[ht:2 * ht]
    kv_ref[0] = col[2 * ht:]


def exchange(axis, me, n, srcs, dst, send_sem, recv_sem):
    copies = []
    for t in range(1, n):
        peer = lax.rem(me + t, n)
        copy = pltpu.make_async_remote_copy(src_ref=srcs(peer), dst_ref=dst.at[me], send_sem=send_sem.at[t],
                                            recv_sem=recv_sem.at[t], device_id={axis: peer}, device_id_type=MESH)
        copy.start()
        copies.append(copy)
    return copies


def col_kernel(axis, n, heads, hd, scale, qsum_ref, cnt_ref, kv_ref, m_ref, o_ref,
               l_ref, qp_ref, qb_ref, st_ref, sp_ref, send_sem, recv_sem):
    ng, _, wide = kv_ref.shape
    res = qsum_ref.shape[1]
    us = wide // res
    ht = heads * hd
    me = lax.axis_index(axis)
    barrier = pltpu.get_barrier_semaphore()
    for t in range(1, n):
        pl.semaphore_signal(barrier, inc=1, device_id={axis: lax.rem(me + t, n)}, device_id_type=MESH)
    pl.semaphore_wait(barrier, n - 1)

    blk = ht // n
    mine = pl.ds(pl.multiple_of(me * blk, blk), blk)
    copies = exchange(axis, me, n, lambda p: qsum_ref.at[pl.ds(pl.multiple_of(p * blk, blk), blk)], qp_ref,
                      send_sem.at[0], recv_sem.at[0])
    qp_ref[me] = qsum_ref[mine]
    for c in copies:
        c.wait()
    tot = qp_ref[0]
    for t in range(1, n):
        tot = tot + qp_ref[t]
    qb_ref[me] = (tot / (cnt_ref[...] + 1e-10)).astype(BF16).astype(F32)
    copies = exchange(axis, me, n, lambda p: qb_ref.at[me], qb_ref, send_sem.at[1], recv_sem.at[1])
    for c in copies:
        c.wait()
    qbar = qb_ref[...].reshape(ht, res)

    def logits(gr, top):
        for u in range(us):
            cols = slice(u * res, (u + 1) * res)
            kv = kv_ref[gr, :, cols].astype(F32)
            acc = qbar[0:heads] * kv[0:1]
            for d in range(1, hd):
                acc = acc + qbar[d * heads:(d + 1) * heads] * kv[d:d + 1]
            acc = jnp.where(m_ref[gr, :, cols] > 0, acc * scale, MASK_FILL)
            l_ref[gr, :, cols] = acc
            top = jnp.maximum(top, acc)
        return top

    top = lax.fori_loop(0, ng, logits, jnp.full((heads, res), -3e38, F32))

    def sums(gr, carry):
        for u in range(us):
            cols = slice(u * res, (u + 1) * res)
            w = jnp.exp(l_ref[gr, :, cols] - top)
            kv = kv_ref[gr, :, cols].astype(F32)
            carry = (carry[0] + w,) + tuple(carry[1 + d] + w * kv[hd + d:hd + d + 1] for d in range(hd))
        return carry

    zero = jnp.zeros((heads, res), F32)
    tot = lax.fori_loop(0, ng, sums, (zero,) * (hd + 1))
    for d in range(hd):
        st_ref[:, d, :] = tot[1 + d]
    st_ref[:, hd, :] = tot[0]
    st_ref[:, hd + 1, :] = top
    for d in range(hd + 2, st_ref.shape[1]):
        st_ref[:, d, :] = zero
    copies = exchange(axis, me, n, lambda p: st_ref.at[p], sp_ref, send_sem.at[2], recv_sem.at[2])
    sp_ref[me] = st_ref[me]
    for c in copies:
        c.wait()
    best = sp_ref[0, hd + 1:hd + 2]
    for t in range(1, n):
        best = jnp.maximum(best, sp_ref[t, hd + 1:hd + 2])
    num = jnp.zeros((hd, res), F32)
    den = jnp.zeros((1, res), F32)
    for t in range(n):
        fac = jnp.exp(sp_ref[t, hd + 1:hd + 2] - best)
        num = num + sp_ref[t, 0:hd] * fac
        den = den + sp_ref[t, hd:hd + 1] * fac
    o_ref[me] = num / den
    copies = exchange(axis, me, n, lambda p: o_ref.at[me], o_ref, send_sem.at[3], recv_sem.at[3])
    for c in copies:
        c.wait()


def tail_kernel(o_ref, e1_ref, g_ref, m_ref, bg_ref, wout_ref, tin_ref, tout_ref, opm_ref, e3_ref, ab_ref, buf_ref):
    ht, res = o_ref.shape
    us = e1_ref.shape[2] // res
    blk = 128
    eye = (lax.broadcasted_iota(jnp.int32, (blk, blk), 0) == lax.broadcasted_iota(jnp.int32, (blk, blk), 1)).astype(BF16)
    o = jnp.concatenate([o_ref[...]] * us, axis=1)
    for gr in range(e1_ref.shape[0]):
        gated = (sigmoid(g_ref[gr].astype(F32) + bg_ref[...]) * o).astype(BF16)
        e2 = (e1_ref[gr].astype(F32) + dot(wout_ref[...], gated)).astype(BF16).astype(F32)
        hid = jnp.maximum(dot(tin_ref[...], norm_rows(e2)), 0.0).astype(BF16)
        e3 = (e2 + dot(tout_ref[...], hid)).astype(BF16)
        ab = dot(opm_ref[...], norm_rows(e3.astype(F32))).astype(BF16).astype(F32) * m_ref[gr]
        for u in range(us):
            for t in range(res // blk):
                at = u * res + t * blk
                e3_ref[gr * us + u, t * blk:(t + 1) * blk, :] = dot_t(eye, e3[:, at:at + blk]).astype(BF16)
            buf_ref[:, gr * us + u, :] = ab[:, u * res:(u + 1) * res]
    ab_ref[...] = buf_ref[...].astype(BF16)


def opm_kernel(odim, a_ref, b_ref, z_ref, ninv_ref, w_ref, bo_ref, out_ref, hi_ref, lo_ref):
    ndev, _, ns, jb = b_ref.shape
    ib = z_ref.shape[0]
    a = a_ref[...]
    for q in range(odim // 2):
        rhs = jnp.concatenate([b_ref[:, 2 * q].reshape(ndev * ns, jb), b_ref[:, 2 * q + 1].reshape(ndev * ns, jb)], axis=1)
        pr = dot(a, rhs)
        hi = pr.astype(BF16)
        lo = (pr - hi.astype(F32)).astype(BF16)
        for val, ref in ((hi, hi_ref), (lo, lo_ref)):
            for i in range(ib):
                for t in range(2):
                    ref[i // 2, (2 * q + t) * odim:(2 * q + t + 1) * odim, (i % 2) * jb:(i % 2 + 1) * jb] = \
                        val[i * odim:(i + 1) * odim, t * jb:(t + 1) * jb]
    for ip in range(ib // 2):
        zt = dot(w_ref[...], hi_ref[ip]) + dot(w_ref[...], lo_ref[ip])
        for t in range(2):
            i = 2 * ip + t
            upd = jnp.transpose(zt[:, t * jb:(t + 1) * jb] * ninv_ref[i])
            out_ref[i] = (z_ref[i].astype(F32) + upd + bo_ref[...]).astype(BF16)


def solution(mesh):
    row_spec = P(('batch', 'seq'))
    rep_spec = P()
    n_seq = mesh.shape['seq']

    def local_block(msa, mask, pair, w_pair_bias, w_row_in, b_row_gate, w_row_out, w_col_in, b_col_gate, w_col_out,
                    w_trans_in, w_trans_out, w_opm_in, w_opm_out, b_opm_out):
        ns, res, ch = msa.shape
        rows = pair.shape[0]
        pd = pair.shape[-1]
        heads = w_pair_bias.shape[1]
        ht = w_row_out.shape[0]
        hd = ht // heads
        odim = w_opm_out.shape[0]
        scale = hd ** -0.5
        params = functools.partial(pltpu.CompilerParams, vmem_limit_bytes=VMEM_LIMIT)

        bias_rows = jnp.einsum('ijc,ch->hij', layer_norm(pair), w_pair_bias, preferred_element_type=F32).astype(BF16)
        packed = jnp.concatenate([bias_rows.reshape(heads * rows, res), mask.astype(BF16)], axis=0)
        packed = lax.all_gather(packed, 'seq', axis=0)
        bias_all = packed[:, :heads * rows].reshape(n_seq, heads, rows, res)
        bias_t = jnp.transpose(bias_all, (1, 3, 0, 2)).reshape(heads // 2, 2, res, res)
        bias_t = jnp.transpose(bias_t, (0, 2, 1, 3)).reshape(heads // 2, res, 2 * res).astype(F32) * LOG2E
        mask_all = packed[:, heads * rows:].reshape(n_seq * ns, res)
        counts = jnp.sum(mask_all.astype(F32), axis=0, keepdims=True)
        me = lax.axis_index('seq')
        mask_mine = lax.dynamic_slice_in_dim(mask_all, me * rows, rows, axis=1)
        ninv = 1.0 / (jnp.einsum('si,sj->ij', mask_mine, mask_all, preferred_element_type=F32) + 1e-3)

        us = SEQS
        ng, wide = ns // us, us * res
        mask_f = mask.astype(F32).reshape(ng, 1, wide)
        perm_q = w_col_in[:, :ht].reshape(ch, heads, hd).transpose(0, 2, 1).reshape(ch, ht)
        cin = jnp.concatenate([perm_q, w_col_in[:, ht:]], axis=1).T
        ncol = cin.shape[0]
        bcg = b_col_gate.reshape(ht, 1).astype(F32)
        brg = b_row_gate.reshape(ht, 1).astype(F32)

        full = lambda *shape: pl.BlockSpec(shape, lambda *g: (0,) * len(shape))
        group = lambda k, r: pl.BlockSpec((k, r, wide), lambda s: (s, 0, 0))
        e1, gate, kv, qsum = pl.pallas_call(
            functools.partial(row_kernel, heads, hd, scale),
            grid=(ng,),
            in_specs=[pl.BlockSpec((us, res, ch), lambda s: (s, 0, 0)), group(1, 1),
                      full(heads // 2, res, 2 * res), full(4 * ht, ch), full(ht, 1), full(ch, ht), full(ncol, ch)],
            out_specs=[group(1, ch), group(1, ht), group(1, 2 * hd), full(ht, res)],
            out_shape=[jax.ShapeDtypeStruct((ng, ch, wide), BF16), jax.ShapeDtypeStruct((ng, ht, wide), BF16),
                       jax.ShapeDtypeStruct((ng, 2 * hd, wide), BF16), jax.ShapeDtypeStruct((ht, res), F32)],
            scratch_shapes=[pltpu.VMEM((us, 2 * ht + 16, heads * res), BF16), pltpu.VMEM((wide, 2 * ht + 16), BF16),
                            pltpu.VMEM((heads // 2, 32, wide), BF16), pltpu.VMEM((ht, wide), F32), pltpu.SMEM((1,), F32)],
            compiler_params=params(dimension_semantics=('arbitrary',)),
            name='row_attention',
        )(msa, mask_f, bias_t, w_row_in.T, brg, w_row_out.T, cin)

        col_o = pl.pallas_call(
            functools.partial(col_kernel, 'seq', n_seq, heads, hd, scale),
            in_specs=[pl.BlockSpec(memory_space=pltpu.VMEM)] * 4,
            out_specs=pl.BlockSpec(memory_space=pltpu.VMEM),
            out_shape=jax.ShapeDtypeStruct((heads, hd, res), F32),
            scratch_shapes=[pltpu.VMEM((ng, heads, wide), F32), pltpu.VMEM((n_seq, ht // n_seq, res), F32),
                            pltpu.VMEM((n_seq, ht // n_seq, res), F32), pltpu.VMEM((heads, 16, res), F32),
                            pltpu.VMEM((n_seq, 16, res), F32), pltpu.SemaphoreType.DMA((4, n_seq)),
                            pltpu.SemaphoreType.DMA((4, n_seq))],
            compiler_params=params(collective_id=0, has_side_effects=True),
            name='col_stats',
        )(qsum, counts, kv, mask_f).reshape(ht, res)

        tb = 16
        e3, ab = pl.pallas_call(
            tail_kernel,
            grid=(ns // tb,),
            in_specs=[full(ht, res), group(tb // us, ch), group(tb // us, ht), group(tb // us, 1),
                      full(ht, 1), full(ch, ht), full(w_trans_in.shape[1], ch), full(ch, w_trans_in.shape[1]),
                      full(2 * odim, ch)],
            out_specs=[pl.BlockSpec((tb, res, ch), lambda s: (s, 0, 0)), pl.BlockSpec((2 * odim, tb, res), lambda s: (0, s, 0))],
            out_shape=[jax.ShapeDtypeStruct((ns, res, ch), BF16), jax.ShapeDtypeStruct((2 * odim, ns, res), BF16)],
            scratch_shapes=[pltpu.VMEM((2 * odim, tb, res), F32)],
            compiler_params=params(dimension_semantics=('arbitrary',)),
            name='tail',
        )(col_o, e1, gate, mask_f, bcg, w_col_out.T, w_trans_in.T, w_trans_out.T, w_opm_in.T)

        b_all = lax.all_gather(ab[odim:], 'seq', axis=0)
        a_own = lax.all_to_all(ab[:odim].reshape(odim, ns, n_seq, rows), 'seq', split_axis=2, concat_axis=0)
        a_own = a_own.reshape(n_seq, odim, ns, rows).transpose(3, 1, 0, 2).reshape(rows * odim, n_seq * ns)
        ib, jb = 8, 128
        wt = w_opm_out.transpose(2, 1, 0).reshape(pd, odim * odim)
        pair_out = pl.pallas_call(
            functools.partial(opm_kernel, odim),
            grid=(res // jb, rows // ib),
            in_specs=[pl.BlockSpec((ib * odim, n_seq * ns), lambda j, i: (i, 0)),
                      pl.BlockSpec((n_seq, odim, ns, jb), lambda j, i: (0, 0, 0, j)),
                      pl.BlockSpec((ib, jb, pd), lambda j, i: (i, j, 0)),
                      pl.BlockSpec((ib, 1, jb), lambda j, i: (i, 0, j)),
                      full(pd, odim * odim), full(1, pd)],
            out_specs=pl.BlockSpec((ib, jb, pd), lambda j, i: (i, j, 0)),
            out_shape=jax.ShapeDtypeStruct((rows, res, pd), BF16),
            scratch_shapes=[pltpu.VMEM((ib // 2, odim * odim, 2 * jb), BF16)] * 2,
            compiler_params=params(dimension_semantics=('arbitrary', 'arbitrary')),
            name='outer_product',
        )(a_own, b_all, pair, ninv.reshape(rows, 1, res), wt, b_opm_out.reshape(1, pd).astype(F32))
        return e3, pair_out

    return jax.shard_map(local_block, mesh=mesh, in_specs=(row_spec, row_spec, row_spec) + (rep_spec,) * 12,
                         out_specs=(row_spec, row_spec), check_vma=False)
```

time: 1280 us -> 349 us (0.27)
  matrix products: 639 us -> 8.24 us
  waiting for transfers between devices: 438 us -> 53.2 us
  Pallas kernels: 0 us -> 193 us
  blocking collectives: 69.1 us -> 0 us
  other arithmetic: 73.9 us -> 15.7 us
  local copies, waits for them, and re-layouts: 36.3 us -> 58.5 us
    dot_general x50 -> x2, matrix products: 412 us -> 8.24 us  [the longest x1 7.93 us: local_block(): jnp.einsum('ijc,ch->hij', layer_norm(pair), w_pair_bias, preferred_elemen...]
    reduce_scatter x2 -> x0, waiting for transfers between devices: 363 us -> none  [the longest x1 363 us: local_block(): lax.psum_scatter(local_pair, 'seq', scatter_dimension=0, tiled=True)]
    sub x16 -> x0, matrix products: 227 us -> none  [attend_block(): attn_probs = jax.nn.softmax(scores, axis=-1).astype(jnp.bfloat16)]
    pallas_call x0 -> x4, Pallas kernels: none -> 193 us  [the longest x1 109 us: local_block(): pl.pallas_call(functools.partial(row_kernel, heads, hd, scale), grid=(ng,...]
    psum x2 -> x0, waiting for transfers between devices: 74.6 us -> none  [the longest x1 48.2 us: local_block(): q_sum, counts = lax.psum((q_sum, counts), 'seq')]
    convert_element_type x21 -> x4, other arithmetic: 48.6 us -> 1.7 us  [the longest x1 1.11 us: local_block(): mask.astype(BF16)]
    psum x2 -> x0, blocking collectives: 42.9 us -> none  [the longest x1 28.3 us: local_block(): lax.psum((local_den * rescale, local_num * rescale[:, :, None]), 'seq')]
    all_to_all x0 -> x1, waiting for transfers between devices: none -> 27.4 us  [local_block(): lax.all_to_all(ab[:odim].reshape(odim, ns, n_seq, rows), 'seq', split_axi...]
  transfers between devices with their start and end apart: 5 -> 3, of which waited for: 3 -> 3; matrix products, arithmetic and copies ran while one was open for 23% -> 14% of each run, Pallas kernels for 0% -> 0%
where the time goes in v1:
time: 349 us; the launch traced here: 348 us
  Pallas kernels  193 us (55%)
  local copies, waits for them, and re-layouts  58.5 us (17%)
  waiting for transfers between devices  53.2 us (15%)
  other arithmetic  15.7 us (4%)
  between operations  14.4 us (4%)
  matrix products  8.24 us (2%)
  starting transfers between devices  4.91 us (1%)
    pallas_call x1, Pallas kernels, local_block(): pl.pallas_call(functools.partial(row_kernel, heads, hd, scale), grid=(ng,...  109 us
    pallas_call x1, Pallas kernels, local_block(): pl.pallas_call(functools.partial(opm_kernel, odim), grid=(res // jb, rows...  40.7 us
    all_to_all x1, waiting for transfers between devices, local_block(): lax.all_to_all(ab[:odim].reshape(odim, ns, n_seq, rows), 'seq', split_axi...  27.4 us
    unnamed x40, local copies, waits for them, and re-layouts  25.1 us
    pallas_call x1, Pallas kernels, local_block(): pl.pallas_call(functools.partial(col_kernel, 'seq', n_seq, heads, hd, sca...  22.3 us
    pallas_call x1, Pallas kernels, local_block(): pl.pallas_call(tail_kernel, grid=(ns // tb,), in_specs=[full(ht, res), gr...  20.9 us
    all_gather x1, waiting for transfers between devices, local_block(): packed = lax.all_gather(packed, 'seq', axis=0)  13.9 us
    all_gather x1, waiting for transfers between devices, local_block(): b_all = lax.all_gather(ab[odim:], 'seq', axis=0)  11.8 us
  transfers between devices with their start and end apart: 3, of which 3 were waited for; matrix products, arithmetic and copies ran while one was open for 14% of the time, Pallas kernels for 0%

profile of v1, /device:TPU:113, one launch (start us, length us, event | category | flops | bytes accessed | tf_op | source)
XLA Modules:
  0.0 348.3 jit_solution(8926584188743089462)
XLA Ops:
  7.3 1.1 fusion.19
  8.4 3.9 %convert_reduce_fusion = f32[48,384]{1,0:T(8,128)S(1)} fusion(bf16[48,384,128]{2,1,0:T(8,128)(2,1)} %z_ref.1), kind=kLoop, calls=%fused_computation.1 | loop fusion | flops 4700160 | bytes 4792320 | tf_op jit(solution)/shard_map/reduce_sum | solution.py:22
  12.3 5.5 %fusion.2 = f32[48,384]{1,0:T(8,128)S(1)} fusion(bf16[48,384,128]{2,1,0:T(8,128)(2,1)S(1)} %copy-done.2, f32[48,384]{1,0:T(8,128)S(1)} %broadcast_multiply_fusion), kind=kLoop, calls=%fused_computation.4 | loop fusion | flops 9418752 | bytes 4866048 | tf_op jit(solution)/shard_map/reduce_sum | solution.py:23
  17.9 7.9 %fusion.11 = bf16[8,48,384]{2,0,1:T(8,128)(2,1)S(1)} fusion(bf16[48,384,128]{2,1,0:T(8,128)(2,1)S(1)} %copy-done.2, f32[48,384]{1,0:T(8,128)S(1)} %add_rsqrt_fusion, f32[48,384]{1,0:T(8,128)S(1)} %broadcast_multiply_fusion, bf16[128,8]{0,1:T(8,128)(2,1)S(1)} %copy-done), kind=kOutput, calls=%fused_computation.11 | convolution fusion | flops 47333376 | bytes 5163008 | tf_op jit(solution)/shard_map/ijc,ch->hij/dot_general | solution.py:280
  27.1 4.7 %copy.73.e_ref = bf16[64,384,64]{2,1,0:T(8,128)(2,1)} copy(bf16[64,384,64]{1,2,0:T(8,128)(2,1)S(1)} %copy-done.3) | data formatting | bytes 6291456 | tf_op args[0]
  38.4 13.9 %all-gather.5.cloned.1.call-done = bf16[3584,384]{1,0:T(8,128)(2,1)} async-done(((bf16[448,384]{1,0:T(8,128)(2,1)}), bf16[3584,384]{1,0:T(8,128)(2,1)}) %all-gather.5.cloned.1.call-update) | async-done | bytes 2752528 | tf_op jit(solution)/shard_map/all_gather | solution.py:282
  52.3 2.1 convert_multiply_fusion
  55.5 2.6 copy.66
  58.1 6.0 %copy.84.bias_ref = f32[4,384,768]{2,1,0:T(8,128)} copy(f32[4,384,768]{1,2,0:T(8,128)} %bitcast.59) | data formatting | bytes 9437184 | tf_op jit(solution)/shard_map/mul | solution.py:285
  64.7 109.5 %row_attention.1 = (bf16[16,64,1536]{2,1,0:T(8,128)(2,1)}, bf16[16,64,1536]{2,1,0:T(8,128)(2,1)}, bf16[16,16,1536]{2,1,0:T(8,128)(2,1)}, f32[64,384]{1,0:T(8,128)}) custom-call(bf16[64,384,64]{2,1,0:T(8,128)(2,1)} %copy.73.e_ref, f32[16,1,1536]{2,1,0:T(1,128)} %reshape.64.m_ref, f32[4,384,768]{2,1,0:T(8,128)} %copy.84.bias_ref, bf16[256,64]{1,0:T(8,128)(2,1)} %bitcast.70, ...), custom_call_target="tpu_custom_call" | custom-call | tf_op jit(solution)/shard_map/row_attention/pallas_call | solution.py:303
  174.2 22.3 %col_stats.1 = f32[8,8,384]{2,1,0:T(8,128)} custom-call(f32[64,384]{1,0:T(8,128)} %get-tuple-element.8.qsum_ref, f32[1,384]{1,0:T(1,128)} %broadcast_in_dim.2.cnt_ref, bf16[16,16,1536]{2,1,0:T(8,128)(2,1)} %get-tuple-element.9.kv_ref, f32[16,1,1536]{2,1,0:T(1,128)} %reshape.64.m_ref), custom_call_target="tpu_custom_call" | custom-call | tf_op jit(solution)/shard_map/col_stats/pallas_call | solution.py:317
  196.5 20.9 %tail.1 = (bf16[64,384,64]{2,1,0:T(8,128)(2,1)}, bf16[64,64,384]{2,1,0:T(8,128)(2,1)}) custom-call(f32[64,384]{1,0:T(8,128)} %bitcast.68, bf16[16,64,1536]{2,1,0:T(8,128)(2,1)} %get-tuple-element.10.e1_ref, bf16[16,64,1536]{2,1,0:T(8,128)(2,1)} %get-tuple-element.11.g_ref, f32[16,1,1536]{2,1,0:T(1,128)} %reshape.64.m_ref, f32[64,1]{1,0:T(8,128)} %copy.78.bg_ref, ...), custom_call_target="tpu_custom_call" | custom-call | tf_op jit(solution)/shard_map/tail/pallas_call | solution.py:331
  217.5 3.4 fusion.18
  220.9 4.6 %broadcast_in_dim_reshape.3 = bf16[1,32,64,8,48]{4,3,2,1,0:T(8,128)(2,1)} reshape(bf16[32,64,384]{2,1,0:T(8,128)(2,1)S(1)} %get-tuple-element.23) | data formatting | bytes 3145728 | tf_op jit(solution)/shard_map/broadcast_in_dim;reshape | solution.py:345
  225.5 5.7 %copy.79 = bf16[1,32,64,8,48]{2,4,1,0,3:T(8,128)(2,1)S(1)} copy(bf16[1,32,64,8,48]{4,3,2,1,0:T(8,128)(2,1)} %broadcast_in_dim_reshape.3) | data formatting | bytes 3145728 | tf_op jit(solution)/shard_map/broadcast_in_dim;reshape | solution.py:345
  231.3 4.5 %reshape.83 = bf16[8,2,49152]{2,1,0:T(2,128)(2,1)} reshape(bf16[8,1,32,48,64]{4,3,2,1,0:T(8,128)(2,1)S(1)} %bitcast.60) | data formatting | bytes 3145728
  235.8 4.6 %all-to-all-start = ((bf16[8,2,49152]{2,1,0:T(2,128)(2,1)}), bf16[8,2,49152]{2,1,0:T(2,128)(2,1)}, u32[]{:S(2)}, u32[]{:S(2)}) async-start(bf16[8,2,49152]{2,1,0:T(2,128)(2,1)} %reshape.83), calls=%async_computation | async-start | bytes 3145728 | tf_op jit(solution)/shard_map/all_to_all | solution.py:345
  243.0 6.7 %copy.83 = bf16[64,384,64]{1,2,0:T(8,128)(2,1)} copy(bf16[64,384,64]{2,1,0:T(8,128)(2,1)} %get-tuple-element.20) | data formatting | bytes 6291456
  250.8 27.4 %all-to-all-done = bf16[8,2,49152]{2,1,0:T(2,128)(2,1)} async-done(((bf16[8,2,49152]{2,1,0:T(2,128)(2,1)}), bf16[8,2,49152]{2,1,0:T(2,128)(2,1)}, u32[]{:S(2)}, u32[]{:S(2)}) %all-to-all-start) | async-done | bytes 1572896 | tf_op jit(solution)/shard_map/all_to_all | solution.py:345
  278.2 5.2 %reshape.84 = bf16[8,1,32,48,64]{4,3,2,1,0:T(8,128)(2,1)S(1)} reshape(bf16[8,2,49152]{2,1,0:T(2,128)(2,1)} %all-to-all-done) | data formatting | bytes 3145728
  284.0 2.0 copy.80
  286.0 3.0 reshape.70.a_ref
  288.9 11.8 %all-gather.7.cloned.1.call-done = bf16[256,64,384]{2,1,0:T(8,128)(2,1)} async-done(((bf16[32,64,384]{2,1,0:T(8,128)(2,1)}), bf16[256,64,384]{2,1,0:T(8,128)(2,1)}) %all-gather.7.cloned.1.call-update) | async-done | bytes 12582928 | tf_op jit(solution)/shard_map/all_gather | solution.py:344
  300.7 40.7 %outer_product.1 = bf16[48,384,128]{2,1,0:T(8,128)(2,1)} custom-call(bf16[1536,512]{1,0:T(8,128)(2,1)} %reshape.70.a_ref, bf16[8,32,64,384]{3,2,1,0:T(8,128)(2,1)} %bitcast.61, bf16[48,384,128]{2,1,0:T(8,128)(2,1)} %z_ref.1, f32[48,1,384]{2,1,0:T(1,128)} %reshape.72.ninv_ref, bf16[128,1024]{1,0:T(8,128)(2,1)} %copy.82.w_ref, f32[1,128]{1,0:T(1,128)} %bitcast_convert_fusion.bo_ref), custom_call_target="tpu_custom_call" | custom-call | tf_op jit(solution)/shard_map/outer_product/pallas_call | solution.py:349
  (62 shorter events, 13.7 us)
Async XLA Ops:
  7.2 10.7 %copy-start = (bf16[128,8]{0,1:T(8,128)(2,1)S(1)}, bf16[128,8]{0,1:T(8,128)(2,1)}, u32[]{:S(2)}) copy-start(bf16[128,8]{0,1:T(8,128)(2,1)} %param.18) | copy-start | bytes 6148
  7.2 45.1 %all-gather.5.cloned.1.call-start = ((), (), s32[]{:S(2)}) async-start(), calls=%async_computation.1 | async-start | bytes 3096576 | tf_op jit(solution)/shard_map/all_gather | solution.py:282
  7.3 5.1 %copy-start.2 = (bf16[48,384,128]{2,1,0:T(8,128)(2,1)S(1)}, bf16[48,384,128]{2,1,0:T(8,128)(2,1)}, u32[]{:S(2)}) copy-start(bf16[48,384,128]{2,1,0:T(8,128)(2,1)} %z_ref.1) | copy-start | bytes 14155780
  17.9 9.1 %copy-start.5 = (bf16[64,144]{1,0:T(8,128)(2,1)S(1)}, bf16[64,144]{1,0:T(8,128)(2,1)}, u32[]{:S(2)}) copy-start(bf16[64,144]{1,0:T(8,128)(2,1)} %param.22) | copy-start | bytes 55300
  17.9 9.2 %copy-start.3 = (bf16[64,384,64]{1,2,0:T(8,128)(2,1)S(1)}, bf16[64,384,64]{1,2,0:T(8,128)(2,1)}, u32[]{:S(2)}) copy-start(bf16[64,384,64]{1,2,0:T(8,128)(2,1)} %param.15) | copy-start | bytes 9437188
  26.7 274.0 %all-gather.7.cloned.1.call-start = ((), (), s32[]{:S(2)}) async-start(), calls=%async_computation.2 | async-start | bytes 14155776 | tf_op jit(solution)/shard_map/all_gather | solution.py:344
  27.0 5.5 %copy-start.6 = (bf16[64,256]{1,0:T(8,128)(2,1)S(1)}, bf16[64,256]{1,0:T(8,128)(2,1)}, u32[]{:S(2)}) copy-start(bf16[64,256]{1,0:T(8,128)(2,1)} %param.19) | copy-start | bytes 98308
  27.0 6.3 %copy-start.11 = (bf16[64]{0:T(256)(128)(2,1)S(1)}, bf16[64]{0:T(256)(128)(2,1)}, u32[]{:S(2)}) copy-start(bf16[64]{0:T(256)(128)(2,1)} %param.20) | copy-start | bytes 388
  27.1 7.0 %copy-start.8 = (bf16[64,64]{1,0:T(8,128)(2,1)S(1)}, bf16[64,64]{1,0:T(8,128)(2,1)}, u32[]{:S(2)}) copy-start(bf16[64,64]{1,0:T(8,128)(2,1)} %param.21) | copy-start | bytes 24580
  27.1 7.7 %slice-start = ((bf16[64,144]{1,0:T(8,128)(2,1)}), bf16[64,64]{1,0:T(8,128)(2,1)S(1)}, s32[]{:S(2)}) async-start(bf16[64,144]{1,0:T(8,128)(2,1)} %param.22), calls=%async_computation.3 | async-start | bytes 32768 | tf_op jit(solution)/shard_map/slice | solution.py:295
  27.1 7.8 %copy-start.12 = (bf16[64]{0:T(256)(128)(2,1)S(1)}, bf16[64]{0:T(256)(128)(2,1)}, u32[]{:S(2)}) copy-start(bf16[64]{0:T(256)(128)(2,1)} %param.23) | copy-start | bytes 388
  27.1 8.6 %copy-start.9 = (bf16[64,64]{1,0:T(8,128)(2,1)S(1)}, bf16[64,64]{1,0:T(8,128)(2,1)}, u32[]{:S(2)}) copy-start(bf16[64,64]{1,0:T(8,128)(2,1)} %param.24) | copy-start | bytes 24580
  27.1 9.3 %copy-start.7 = (bf16[64,256]{1,0:T(8,128)(2,1)S(1)}, bf16[64,256]{1,0:T(8,128)(2,1)}, u32[]{:S(2)}) copy-start(bf16[64,256]{1,0:T(8,128)(2,1)} %param.25) | copy-start | bytes 98308
  27.1 10.0 %copy-start.10 = (bf16[64,64]{1,0:T(8,128)(2,1)S(1)}, bf16[64,64]{1,0:T(8,128)(2,1)}, u32[]{:S(2)}) copy-start(bf16[64,64]{1,0:T(8,128)(2,1)} %param.27) | copy-start | bytes 24580
  231.3 9.1 %copy-start.4 = (bf16[32,32,128]{2,1,0:T(8,128)(2,1)S(1)}, bf16[32,32,128]{2,1,0:T(8,128)(2,1)}, u32[]{:S(2)}) copy-start(bf16[32,32,128]{2,1,0:T(8,128)(2,1)} %param.28) | copy-start | bytes 786436
  231.3 10.1 %copy-start.13 = (bf16[128]{0:T(256)(128)(2,1)S(1)}, bf16[128]{0:T(256)(128)(2,1)}, u32[]{:S(2)}) copy-start(bf16[128]{0:T(256)(128)(2,1)} %param.29) | copy-start | bytes 772
  235.8 42.4 %all-to-all-start = ((bf16[8,2,49152]{2,1,0:T(2,128)(2,1)}), bf16[8,2,49152]{2,1,0:T(2,128)(2,1)}, u32[]{:S(2)}, u32[]{:S(2)}) async-start(bf16[8,2,49152]{2,1,0:T(2,128)(2,1)} %reshape.83), calls=%async_computation | async-start | bytes 3145728 | tf_op jit(solution)/shard_map/all_to_all | solution.py:345
  300.7 40.7 %copy-start.1 = (bf16[128,8]{0,1:T(8,128)(2,1)S(1)}, bf16[128,8]{0,1:T(8,128)(2,1)}, u32[]{:S(2)}) copy-start(bf16[128,8]{0,1:T(8,128)(2,1)} %param.18) | copy-start | bytes 6148
Sparse Core Ops, SparseCore 0:
  26.8 25.4 all-gather.4
  221.0 79.6 all-gather.6

commit v2 on v1

--- a/solution.py
+++ b/solution.py
@@ -17,13 +17,6 @@
 SEQS = 4
 
 
-def layer_norm(values):
-    as_float = values.astype(F32)
-    centered = as_float - jnp.mean(as_float, axis=-1, keepdims=True)
-    variance = jnp.mean(centered * centered, axis=-1, keepdims=True)
-    return (centered * lax.rsqrt(variance + 1e-5)).astype(BF16)
-
-
 def norm_rows(x):
     c = x - jnp.mean(x, axis=0, keepdims=True)
     var = jnp.mean(c * c, axis=0, keepdims=True)
@@ -46,9 +39,97 @@
     return jnp.max(jnp.max(x, axis=0, keepdims=True), axis=1, keepdims=True)[0, 0]
 
 
-def row_kernel(heads, hd, scale, e_ref, m_ref, bias_ref, win_ref, bg_ref, wout_ref, cin_ref,
-               e1_ref, g_ref, kv_ref, qsum_ref, rhs_ref, kaug_ref, va_ref, att_ref, top_ref):
-    us, res, ch = e_ref.shape
+def enter(axis, me, n):
+    barrier = pltpu.get_barrier_semaphore()
+    for t in range(1, n):
+        pl.semaphore_signal(barrier, inc=1, device_id={axis: lax.rem(me + t, n)}, device_id_type=MESH)
+    pl.semaphore_wait(barrier, n - 1)
+
+
+def neighbours(me, n):
+    return lax.rem(me + 2, n), lax.rem(me + n - 2, n), lax.rem(me + 4, n), me + 1 - 2 * lax.rem(me, 2)
+
+
+def sender(axis, send_sem, recv_sem):
+    def send(k, src, dst, to):
+        copy = pltpu.make_async_remote_copy(src_ref=src, dst_ref=dst, send_sem=send_sem.at[k], recv_sem=recv_sem.at[k],
+                                            device_id={axis: to}, device_id_type=MESH)
+        copy.start()
+        return copy
+    return send
+
+
+def gather_open(send, me, n, own, buf):
+    right, left, _, other = neighbours(me, n)
+    return [send(0, own, buf.at[me], right), send(1, own, buf.at[me], left), send(2, own, buf.at[me], other)]
+
+
+def gather_pass(send, me, n, buf, half, c):
+    right, left, _, other = neighbours(me, n)
+    c[0].wait_recv()
+    c.append(send(3, buf.at[left, 0:half], buf.at[left, 0:half], right))
+    c.append(send(5, buf.at[left], buf.at[left], other))
+    c[1].wait_recv()
+    c.append(send(4, buf.at[right, half:], buf.at[right, half:], left))
+    c.append(send(6, buf.at[right], buf.at[right], other))
+    return c
+
+
+def gather_close(send, me, n, buf, half, c):
+    _, _, far, other = neighbours(me, n)
+    c[3].wait_recv()
+    c.append(send(7, buf.at[far, 0:half], buf.at[far, 0:half], other))
+    c[5].wait_recv()
+    c.append(send(8, buf.at[far, half:], buf.at[far, half:], other))
+    for t in (2, 4, 6, 7, 8):
+        c[t].wait_recv()
+    for t in c:
+        t.wait_send()
+
+
+def identity(size):
+    return (lax.broadcasted_iota(jnp.int32, (size, size), 0) == lax.broadcasted_iota(jnp.int32, (size, size), 1)).astype(BF16)
+
+
+def bias_kernel(axis, n, z_ref, w_ref, m_ref, out_ref, ninv_ref, cnt_ref, blk_ref, send_sem, recv_sem):
+    rows, res, pd = z_ref.shape
+    heads = w_ref.shape[0]
+    ns = m_ref.shape[0]
+    me = lax.axis_index(axis)
+    enter(axis, me, n)
+    eye = identity(pd)
+    tall, step = 16, 4
+
+    def block(ib, _):
+        for t in range(tall // step):
+            zt = dot_t(eye, z_ref[pl.ds(ib * tall + t * step, step)].reshape(step * res, pd))
+            b = dot(w_ref[...], norm_rows(zt))
+            for u in range(step):
+                blk_ref[:, t * step + u, :] = b[:, u * res:(u + 1) * res]
+        for h in range(heads):
+            out_ref[me, pl.ds(pl.multiple_of(h * rows + ib * tall, tall), tall), :] = blk_ref[h].astype(BF16)
+        return 0
+
+    lax.fori_loop(0, rows // tall, block, 0)
+    out_ref[me, heads * rows:, :] = m_ref[...]
+    half = out_ref.shape[1] // 2
+    send = sender(axis, send_sem, recv_sem)
+    c = gather_open(send, me, n, out_ref.at[me], out_ref)
+    c = gather_pass(send, me, n, out_ref, half, c)
+    gather_close(send, me, n, out_ref, half, c)
+    mask = out_ref[:, heads * rows:, :].reshape(n * ns, res)
+    pick = (lax.broadcasted_iota(jnp.int32, (rows, res), 1) ==
+            lax.broadcasted_iota(jnp.int32, (rows, res), 0) + me * rows).astype(BF16)
+    pairs = dot(dot_t(pick, mask).astype(BF16), mask)
+    ninv = 1.0 / (pairs + 1e-3)
+    for i in range(rows):
+        ninv_ref[i] = ninv[i:i + 1]
+    cnt_ref[...] = dot(jnp.ones((8, n * ns), BF16), mask)[0:1]
+
+
+def row_kernel(heads, hd, scale, e_ref, m_ref, packed_ref, win_ref, bg_ref, wout_ref, cin_ref,
+               e1_ref, g_ref, kv_ref, qsum_ref, rhs_ref, kaug_ref, va_ref, att_ref, bias_ref, top_ref):
+    us, ch, res = e_ref.shape
     ht = heads * hd
     wide = us * res
     step = pl.program_id(0)
@@ -58,13 +139,16 @@
         rows = lax.broadcasted_iota(jnp.int32, rhs_ref.shape, 1)
         rhs_ref[...] = jnp.where(rows == 2 * ht, 1.0, 0.0).astype(BF16)
         qsum_ref[...] = jnp.zeros_like(qsum_ref)
+        n, rows = packed_ref.shape[0], res // packed_ref.shape[0]
+        for h in range(heads):
+            one = jnp.concatenate([packed_ref[d, h * rows:(h + 1) * rows, :] for d in range(n)], axis=0)
+            bias_ref[h // 2, :, (h % 2) * res:(h % 2 + 1) * res] = jnp.transpose(one.astype(F32)) * LOG2E
         top = jnp.abs(bias_ref[0])
         for pr in range(1, heads // 2):
             top = jnp.maximum(top, jnp.abs(bias_ref[pr]))
         top_ref[0] = wide_max(top)
 
-    eye = (lax.broadcasted_iota(jnp.int32, (ch, ch), 0) == lax.broadcasted_iota(jnp.int32, (ch, ch), 1)).astype(BF16)
-    x = dot_t(eye, e_ref[...].reshape(wide, ch))
+    x = jnp.concatenate([e_ref[u] for u in range(us)], axis=1).astype(F32)
     proj = dot(win_ref[...], norm_rows(x)).astype(BF16).astype(F32)
     q, k, v, g = (proj[n * ht:(n + 1) * ht] for n in range(4))
     keep = m_ref[0]
@@ -148,11 +232,7 @@
     us = wide // res
     ht = heads * hd
     me = lax.axis_index(axis)
-    barrier = pltpu.get_barrier_semaphore()
-    for t in range(1, n):
-        pl.semaphore_signal(barrier, inc=1, device_id={axis: lax.rem(me + t, n)}, device_id_type=MESH)
-    pl.semaphore_wait(barrier, n - 1)
-
+    enter(axis, me, n)
     blk = ht // n
     mine = pl.ds(pl.multiple_of(me * blk, blk), blk)
     copies = exchange(axis, me, n, lambda p: qsum_ref.at[pl.ds(pl.multiple_of(p * blk, blk), blk)], qp_ref,
@@ -218,11 +298,12 @@
         c.wait()
 
 
-def tail_kernel(o_ref, e1_ref, g_ref, m_ref, bg_ref, wout_ref, tin_ref, tout_ref, opm_ref, e3_ref, ab_ref, buf_ref):
+def tail_kernel(rows, o_ref, e1_ref, g_ref, m_ref, bg_ref, wout_ref, tin_ref, tout_ref, opm_ref,
+                e3_ref, a_ref, b_ref, buf_ref):
     ht, res = o_ref.shape
     us = e1_ref.shape[2] // res
-    blk = 128
-    eye = (lax.broadcasted_iota(jnp.int32, (blk, blk), 0) == lax.broadcasted_iota(jnp.int32, (blk, blk), 1)).astype(BF16)
+    tb = e3_ref.shape[0]
+    chips, odim, _, blk = a_ref.shape
     o = jnp.concatenate([o_ref[...]] * us, axis=1)
     for gr in range(e1_ref.shape[0]):
         gated = (sigmoid(g_ref[gr].astype(F32) + bg_ref[...]) * o).astype(BF16)
@@ -231,33 +312,98 @@
         e3 = (e2 + dot(tout_ref[...], hid)).astype(BF16)
         ab = dot(opm_ref[...], norm_rows(e3.astype(F32))).astype(BF16).astype(F32) * m_ref[gr]
         for u in range(us):
-            for t in range(res // blk):
-                at = u * res + t * blk
-                e3_ref[gr * us + u, t * blk:(t + 1) * blk, :] = dot_t(eye, e3[:, at:at + blk]).astype(BF16)
-            buf_ref[:, gr * us + u, :] = ab[:, u * res:(u + 1) * res]
-    ab_ref[...] = buf_ref[...].astype(BF16)
-
-
-def opm_kernel(odim, a_ref, b_ref, z_ref, ninv_ref, w_ref, bo_ref, out_ref, hi_ref, lo_ref):
-    ndev, _, ns, jb = b_ref.shape
-    ib = z_ref.shape[0]
-    a = a_ref[...]
-    for q in range(odim // 2):
-        rhs = jnp.concatenate([b_ref[:, 2 * q].reshape(ndev * ns, jb), b_ref[:, 2 * q + 1].reshape(ndev * ns, jb)], axis=1)
-        pr = dot(a, rhs)
-        hi = pr.astype(BF16)
-        lo = (pr - hi.astype(F32)).astype(BF16)
-        for val, ref in ((hi, hi_ref), (lo, lo_ref)):
-            for i in range(ib):
-                for t in range(2):
-                    ref[i // 2, (2 * q + t) * odim:(2 * q + t + 1) * odim, (i % 2) * jb:(i % 2 + 1) * jb] = \
-                        val[i * odim:(i + 1) * odim, t * jb:(t + 1) * jb]
-    for ip in range(ib // 2):
-        zt = dot(w_ref[...], hi_ref[ip]) + dot(w_ref[...], lo_ref[ip])
-        for t in range(2):
-            i = 2 * ip + t
-            upd = jnp.transpose(zt[:, t * jb:(t + 1) * jb] * ninv_ref[i])
-            out_ref[i] = (z_ref[i].astype(F32) + upd + bo_ref[...]).astype(BF16)
+            cols = slice(u * res, (u + 1) * res)
+            e3_ref[gr * us + u] = e3[:, cols]
+            buf_ref[:, gr * us + u, :] = ab[:, cols]
+    for t in range(res // blk):
+        b_ref[t] = buf_ref[odim:, :, t * blk:(t + 1) * blk].astype(BF16)
+    src = lax.broadcasted_iota(jnp.int32, (res, chips * blk), 0)
+    dst = lax.broadcasted_iota(jnp.int32, (res, chips * blk), 1)
+    half = blk // 2
+    place = ((dst % half < rows) & (src == (dst // half) * rows + dst % half)).astype(BF16)
+    moved = dot(buf_ref[0:odim].astype(BF16).reshape(odim * tb, res), place).astype(BF16)
+    for c in range(chips):
+        a_ref[c] = moved[:, c * blk:(c + 1) * blk].reshape(odim, tb, blk)
+
+
+def opm_kernel(axis, n, a_ref, b_ref, z_ref, ninv_ref, w_ref, bo_ref, out_ref,
+               ag_ref, tr_ref, bg_ref, at_ref, hi_ref, lo_ref, asend, arecv, bsend, brecv):
+    rows, res, pd = z_ref.shape
+    nb, odim, ns, jb = b_ref.shape
+    chips = a_ref.shape[0]
+    ib = 2 * hi_ref.shape[0]
+    me = lax.axis_index(axis)
+    chip, core = me // 2, lax.rem(me, 2)
+    right, left, far, other = neighbours(me, n)
+    enter(axis, me, n)
+    half = odim // 2
+    sa = sender(axis, asend, arecv)
+    sb = [sender(axis, bsend.at[t], brecv.at[t]) for t in range(nb)]
+    up, down, across = lax.rem(chip + 1, chips), lax.rem(chip + chips - 1, chips), lax.rem(chip + 2, chips)
+    ca = [sa(2, a_ref.at[across, 0:half], tr_ref.at[0], right), sa(3, a_ref.at[across, half:], tr_ref.at[1], left),
+          sa(0, a_ref.at[up], ag_ref.at[me], right), sa(1, a_ref.at[down], ag_ref.at[me], left),
+          sa(4, a_ref.at[chip], ag_ref.at[me], other)]
+    cb = [gather_open(sb[0], me, n, b_ref.at[0], bg_ref.at[0])]
+    ag_ref[me] = a_ref[chip]
+    for t in range(nb):
+        bg_ref[t, me] = b_ref[t]
+    ca[0].wait_recv()
+    ca.append(sa(5, tr_ref.at[0], ag_ref.at[left, 0:half], right))
+    ca[1].wait_recv()
+    ca.append(sa(6, tr_ref.at[1], ag_ref.at[right, half:], left))
+    ca[2].wait_recv()
+    ca.append(sa(7, ag_ref.at[left], ag_ref.at[left], other))
+    ca[3].wait_recv()
+    ca.append(sa(8, ag_ref.at[right], ag_ref.at[right], other))
+    cb[0] = gather_pass(sb[0], me, n, bg_ref.at[0], half, cb[0])
+    cb.append(gather_open(sb[1], me, n, b_ref.at[1], bg_ref.at[1]))
+    ca[5].wait_recv()
+    ca.append(sa(9, ag_ref.at[far, 0:half], ag_ref.at[far, 0:half], other))
+    ca[6].wait_recv()
+    ca.append(sa(10, ag_ref.at[far, half:], ag_ref.at[far, half:], other))
+    for t in (4, 7, 8, 9, 10):
+        ca[t].wait_recv()
+    pick = (lax.broadcasted_iota(jnp.int32, (rows, jb), 1) ==
+            lax.broadcasted_iota(jnp.int32, (rows, jb), 0) + core * (jb // 2)).astype(BF16)
+    for c in range(odim):
+        at_ref[:, c, :] = dot_t(pick, ag_ref[:, c].reshape(n * ns, jb))
+
+    def tile(t):
+        cols = slice(t * jb, (t + 1) * jb)
+
+        def body(k, _):
+            base = k * ib
+            a = at_ref[pl.ds(base, ib)].reshape(ib * odim, n * ns).astype(BF16)
+            for q in range(odim // 2):
+                rhs = jnp.concatenate([bg_ref[t, :, 2 * q].reshape(n * ns, jb), bg_ref[t, :, 2 * q + 1].reshape(n * ns, jb)], axis=1)
+                pr = dot(a, rhs)
+                hi = pr.astype(BF16)
+                lo = (pr - hi.astype(F32)).astype(BF16)
+                for val, ref in ((hi, hi_ref), (lo, lo_ref)):
+                    for i in range(ib):
+                        for h in range(2):
+                            ref[i // 2, (2 * q + h) * odim:(2 * q + h + 1) * odim, (i % 2) * jb:(i % 2 + 1) * jb] = \
+                                val[i * odim:(i + 1) * odim, h * jb:(h + 1) * jb]
+            for ip in range(ib // 2):
+                zt = dot(w_ref[...], hi_ref[ip]) + dot(w_ref[...], lo_ref[ip])
+                for h in range(2):
+                    i = base + 2 * ip + h
+                    upd = jnp.transpose(zt[:, h * jb:(h + 1) * jb] * ninv_ref[i, :, cols])
+                    out_ref[i, cols, :] = (z_ref[i, cols, :].astype(F32) + upd + bo_ref[...]).astype(BF16)
+            return 0
+
+        lax.fori_loop(0, rows // ib, body, 0)
+
+    gather_close(sb[0], me, n, bg_ref.at[0], half, cb[0])
+    for t in range(1, nb):
+        if t + 1 < nb:
+            cb.append(gather_open(sb[t + 1], me, n, b_ref.at[t + 1], bg_ref.at[t + 1]))
+        tile(t - 1)
+        cb[t] = gather_pass(sb[t], me, n, bg_ref.at[t], half, cb[t])
+        gather_close(sb[t], me, n, bg_ref.at[t], half, cb[t])
+    tile(nb - 1)
+    for t in ca:
+        t.wait_send()
 
 
 def solution(mesh):
@@ -277,17 +423,18 @@
         scale = hd ** -0.5
         params = functools.partial(pltpu.CompilerParams, vmem_limit_bytes=VMEM_LIMIT)
 
-        bias_rows = jnp.einsum('ijc,ch->hij', layer_norm(pair), w_pair_bias, preferred_element_type=F32).astype(BF16)
-        packed = jnp.concatenate([bias_rows.reshape(heads * rows, res), mask.astype(BF16)], axis=0)
-        packed = lax.all_gather(packed, 'seq', axis=0)
-        bias_all = packed[:, :heads * rows].reshape(n_seq, heads, rows, res)
-        bias_t = jnp.transpose(bias_all, (1, 3, 0, 2)).reshape(heads // 2, 2, res, res)
-        bias_t = jnp.transpose(bias_t, (0, 2, 1, 3)).reshape(heads // 2, res, 2 * res).astype(F32) * LOG2E
-        mask_all = packed[:, heads * rows:].reshape(n_seq * ns, res)
-        counts = jnp.sum(mask_all.astype(F32), axis=0, keepdims=True)
-        me = lax.axis_index('seq')
-        mask_mine = lax.dynamic_slice_in_dim(mask_all, me * rows, rows, axis=1)
-        ninv = 1.0 / (jnp.einsum('si,sj->ij', mask_mine, mask_all, preferred_element_type=F32) + 1e-3)
+        vm = pl.BlockSpec(memory_space=pltpu.VMEM)
+        width = heads * rows + ns
+        packed, ninv, counts = pl.pallas_call(
+            functools.partial(bias_kernel, 'seq', n_seq),
+            in_specs=[vm] * 3,
+            out_specs=[vm] * 3,
+            out_shape=[jax.ShapeDtypeStruct((n_seq, width, res), BF16), jax.ShapeDtypeStruct((rows, 1, res), F32),
+                       jax.ShapeDtypeStruct((1, res), F32)],
+            scratch_shapes=[pltpu.VMEM((heads, 16, res), F32), pltpu.SemaphoreType.DMA((9,)), pltpu.SemaphoreType.DMA((9,))],
+            compiler_params=params(collective_id=1, has_side_effects=True),
+            name='pair_bias',
+        )(pair, w_pair_bias.T, mask.astype(BF16))
 
         us = SEQS
         ng, wide = ns // us, us * res
@@ -303,16 +450,17 @@
         e1, gate, kv, qsum = pl.pallas_call(
             functools.partial(row_kernel, heads, hd, scale),
             grid=(ng,),
-            in_specs=[pl.BlockSpec((us, res, ch), lambda s: (s, 0, 0)), group(1, 1),
-                      full(heads // 2, res, 2 * res), full(4 * ht, ch), full(ht, 1), full(ch, ht), full(ncol, ch)],
+            in_specs=[pl.BlockSpec((us, ch, res), lambda s: (s, 0, 0)), group(1, 1),
+                      full(n_seq, width, res), full(4 * ht, ch), full(ht, 1), full(ch, ht), full(ncol, ch)],
             out_specs=[group(1, ch), group(1, ht), group(1, 2 * hd), full(ht, res)],
             out_shape=[jax.ShapeDtypeStruct((ng, ch, wide), BF16), jax.ShapeDtypeStruct((ng, ht, wide), BF16),
                        jax.ShapeDtypeStruct((ng, 2 * hd, wide), BF16), jax.ShapeDtypeStruct((ht, res), F32)],
             scratch_shapes=[pltpu.VMEM((us, 2 * ht + 16, heads * res), BF16), pltpu.VMEM((wide, 2 * ht + 16), BF16),
-                            pltpu.VMEM((heads // 2, 32, wide), BF16), pltpu.VMEM((ht, wide), F32), pltpu.SMEM((1,), F32)],
+                            pltpu.VMEM((heads // 2, 32, wide), BF16), pltpu.VMEM((ht, wide), F32),
+                            pltpu.VMEM((heads // 2, res, 2 * res), F32), pltpu.SMEM((1,), F32)],
             compiler_params=params(dimension_semantics=('arbitrary',)),
             name='row_attention',
-        )(msa, mask_f, bias_t, w_row_in.T, brg, w_row_out.T, cin)
+        )(jnp.transpose(msa, (0, 2, 1)), mask_f, packed, w_row_in.T, brg, w_row_out.T, cin)
 
         col_o = pl.pallas_call(
             functools.partial(col_kernel, 'seq', n_seq, heads, hd, scale),
@@ -327,40 +475,39 @@
             name='col_stats',
         )(qsum, counts, kv, mask_f).reshape(ht, res)
 
-        tb = 16
-        e3, ab = pl.pallas_call(
-            tail_kernel,
+        tb, jb, ib = 16, 128, 8
+        chips = n_seq // 2
+        e3, a_part, b_part = pl.pallas_call(
+            functools.partial(tail_kernel, rows),
             grid=(ns // tb,),
             in_specs=[full(ht, res), group(tb // us, ch), group(tb // us, ht), group(tb // us, 1),
                       full(ht, 1), full(ch, ht), full(w_trans_in.shape[1], ch), full(ch, w_trans_in.shape[1]),
                       full(2 * odim, ch)],
-            out_specs=[pl.BlockSpec((tb, res, ch), lambda s: (s, 0, 0)), pl.BlockSpec((2 * odim, tb, res), lambda s: (0, s, 0))],
-            out_shape=[jax.ShapeDtypeStruct((ns, res, ch), BF16), jax.ShapeDtypeStruct((2 * odim, ns, res), BF16)],
+            out_specs=[pl.BlockSpec((tb, ch, res), lambda s: (s, 0, 0)),
+                       pl.BlockSpec((chips, odim, tb, jb), lambda s: (0, 0, s, 0)),
+                       pl.BlockSpec((res // jb, odim, tb, jb), lambda s: (0, 0, s, 0))],
+            out_shape=[jax.ShapeDtypeStruct((ns, ch, res), BF16), jax.ShapeDtypeStruct((chips, odim, ns, jb), BF16),
+                       jax.ShapeDtypeStruct((res // jb, odim, ns, jb), BF16)],
             scratch_shapes=[pltpu.VMEM((2 * odim, tb, res), F32)],
             compiler_params=params(dimension_semantics=('arbitrary',)),
             name='tail',
         )(col_o, e1, gate, mask_f, bcg, w_col_out.T, w_trans_in.T, w_trans_out.T, w_opm_in.T)
 
-        b_all = lax.all_gather(ab[odim:], 'seq', axis=0)
-        a_own = lax.all_to_all(ab[:odim].reshape(odim, ns, n_seq, rows), 'seq', split_axis=2, concat_axis=0)
-        a_own = a_own.reshape(n_seq, odim, ns, rows).transpose(3, 1, 0, 2).reshape(rows * odim, n_seq * ns)
-        ib, jb = 8, 128
         wt = w_opm_out.transpose(2, 1, 0).reshape(pd, odim * odim)
         pair_out = pl.pallas_call(
-            functools.partial(opm_kernel, odim),
-            grid=(res // jb, rows // ib),
-            in_specs=[pl.BlockSpec((ib * odim, n_seq * ns), lambda j, i: (i, 0)),
-                      pl.BlockSpec((n_seq, odim, ns, jb), lambda j, i: (0, 0, 0, j)),
-                      pl.BlockSpec((ib, jb, pd), lambda j, i: (i, j, 0)),
-                      pl.BlockSpec((ib, 1, jb), lambda j, i: (i, 0, j)),
-                      full(pd, odim * odim), full(1, pd)],
-            out_specs=pl.BlockSpec((ib, jb, pd), lambda j, i: (i, j, 0)),
+            functools.partial(opm_kernel, 'seq', n_seq),
+            in_specs=[vm] * 6,
+            out_specs=vm,
             out_shape=jax.ShapeDtypeStruct((rows, res, pd), BF16),
-            scratch_shapes=[pltpu.VMEM((ib // 2, odim * odim, 2 * jb), BF16)] * 2,
-            compiler_params=params(dimension_semantics=('arbitrary', 'arbitrary')),
+            scratch_shapes=[pltpu.VMEM((n_seq, odim, ns, jb), BF16), pltpu.VMEM((2, odim // 2, ns, jb), BF16),
+                            pltpu.VMEM((res // jb, n_seq, odim, ns, jb), BF16), pltpu.VMEM((rows, odim, n_seq * ns), F32),
+                            pltpu.VMEM((ib // 2, odim * odim, 2 * jb), BF16), pltpu.VMEM((ib // 2, odim * odim, 2 * jb), BF16),
+                            pltpu.SemaphoreType.DMA((11,)), pltpu.SemaphoreType.DMA((11,)),
+                            pltpu.SemaphoreType.DMA((res // jb, 9)), pltpu.SemaphoreType.DMA((res // jb, 9))],
+            compiler_params=params(collective_id=2, has_side_effects=True),
             name='outer_product',
-        )(a_own, b_all, pair, ninv.reshape(rows, 1, res), wt, b_opm_out.reshape(1, pd).astype(F32))
-        return e3, pair_out
+        )(a_part, b_part, pair, ninv, wt, b_opm_out.reshape(1, pd).astype(F32))
+        return jnp.transpose(e3, (0, 2, 1)), pair_out
 
     return jax.shard_map(local_block, mesh=mesh, in_specs=(row_spec, row_spec, row_spec) + (rep_spec,) * 12,
                          out_specs=(row_spec, row_spec), check_vma=False)

time: 349 us -> 308 us (0.88)
  Pallas kernels: 193 us -> 292 us
  waiting for transfers between devices: 53.2 us -> 0 us
  local copies, waits for them, and re-layouts: 58.5 us -> 12 us
  between operations: 14.4 us -> 0.75 us
  other arithmetic: 15.7 us -> 2.77 us
  matrix products: 8.24 us -> 0 us
  starting transfers between devices: 4.91 us -> 0 us
    pallas_call x2 -> x3, Pallas kernels: 61.6 us -> 163 us  [the longest x1 113 us: local_block(): pl.pallas_call(functools.partial(opm_kernel, 'seq', n_seq), in_specs=[vm]...]
    all_to_all x1 -> x0, waiting for transfers between devices: 27.4 us -> none  [local_block(): lax.all_to_all(ab[:odim].reshape(odim, ns, n_seq, rows), 'seq', split_axi...]
    all_gather x2 -> x0, waiting for transfers between devices: 25.7 us -> none  [the longest x1 13.9 us: local_block(): packed = lax.all_gather(packed, 'seq', axis=0)]
    unnamed x40 -> x29, local copies, waits for them, and re-layouts: 25.1 us -> 8.9 us
    reduce_sum x3 -> x0, other arithmetic: 10.5 us -> none  [the longest x1 5.47 us: layer_norm(): variance = jnp.mean(centered * centered, axis=-1, keepdims=True)]
    another operation x2 -> x0, local copies, waits for them, and re-layouts: 10.3 us -> none  [local_block(): lax.all_to_all(ab[:odim].reshape(odim, ns, n_seq, rows), 'seq', split_axi...]
    mul x2 -> x0, local copies, waits for them, and re-layouts: 8.67 us -> none  [local_block(): jnp.transpose(bias_t, (0, 2, 1, 3)).reshape(heads // 2, res, 2 * res)]
    dot_general x2 -> x0, matrix products: 8.24 us -> none  [the longest x1 7.93 us: local_block(): jnp.einsum('ijc,ch->hij', layer_norm(pair), w_pair_bias, preferred_elemen...]
  transfers between devices with their start and end apart: 3 -> 0, of which waited for: 3 -> 0; matrix products, arithmetic and copies ran while one was open for 14% -> 0% of each run, Pallas kernels for 0% -> 0%
where the time goes in v2:
time: 308 us
  Pallas kernels  292 us (95%)
  local copies, waits for them, and re-layouts  12 us (4%)
    pallas_call x1, Pallas kernels, local_block(): pl.pallas_call(functools.partial(opm_kernel, 'seq', n_seq), in_specs=[vm]...  113 us
    pallas_call x1, Pallas kernels, local_block(): pl.pallas_call(functools.partial(row_kernel, heads, hd, scale), grid=(ng,...  107 us
    pallas_call x1, Pallas kernels, local_block(): pl.pallas_call(functools.partial(bias_kernel, 'seq', n_seq), in_specs=[vm...  29.5 us
    pallas_call x1, Pallas kernels, local_block(): pl.pallas_call(functools.partial(col_kernel, 'seq', n_seq, heads, hd, sca...  22.5 us
    pallas_call x1, Pallas kernels, local_block(): pl.pallas_call(functools.partial(tail_kernel, rows), grid=(ns // tb,), in...  20.3 us
    unnamed x29, local copies, waits for them, and re-layouts  8.9 us

profile of v2, /device:TPU:113, one launch (start us, length us, event | category | flops | bytes accessed | tf_op | source)
XLA Modules:
  0.0 307.9 jit_solution(8150583005437824820)
XLA Ops:
  0.6 0.0 slice-start
  0.7 1.6 fusion
  2.3 29.5 %pair_bias.1 = (bf16[8,448,384]{2,1,0:T(8,128)(2,1)}, f32[48,1,384]{2,1,0:T(1,128)}, f32[1,384]{1,0:T(1,128)}) custom-call(bf16[48,384,128]{2,1,0:T(8,128)(2,1)} %z_ref.3, bf16[8,128]{1,0:T(8,128)(2,1)} %bitcast.41, bf16[64,384]{1,0:T(8,128)(2,1)} %get-tuple-element.22.m_ref), custom_call_target="tpu_custom_call" | custom-call | tf_op jit(solution)/shard_map/pair_bias/pallas_call | solution.py:428
  31.8 0.7 reshape.28.m_ref
  32.6 0.0 slice-done
  32.6 0.1 copy.39
  32.7 0.1 slice.7
  32.8 0.1 copy.40
  32.9 0.6 maximum_bitcast_fusion.cin_ref
  33.5 0.7 copy.27
  34.2 0.7 copy.32.bg_ref
  34.9 0.7 copy.28
  35.7 107.2 %row_attention.1 = (bf16[16,64,1536]{2,1,0:T(8,128)(2,1)}, bf16[16,64,1536]{2,1,0:T(8,128)(2,1)}, bf16[16,16,1536]{2,1,0:T(8,128)(2,1)}, f32[64,384]{1,0:T(8,128)}) custom-call(bf16[64,64,384]{2,1,0:T(8,128)(2,1)} %bitcast.30, f32[16,1,1536]{2,1,0:T(1,128)} %reshape.28.m_ref, bf16[8,448,384]{2,1,0:T(8,128)(2,1)} %get-tuple-element.12.packed_ref, ...), custom_call_target="tpu_custom_call" | custom-call | tf_op jit(solution)/shard_map/row_attention/pallas_call | solution.py:450
  142.8 22.5 %col_stats.1 = f32[8,8,384]{2,1,0:T(8,128)} custom-call(f32[64,384]{1,0:T(8,128)} %get-tuple-element.13.qsum_ref, f32[1,384]{1,0:T(1,128)} %get-tuple-element.14.cnt_ref, bf16[16,16,1536]{2,1,0:T(8,128)(2,1)} %get-tuple-element.15.kv_ref, f32[16,1,1536]{2,1,0:T(1,128)} %reshape.28.m_ref), custom_call_target="tpu_custom_call" | custom-call | tf_op jit(solution)/shard_map/col_stats/pallas_call | solution.py:465
  165.3 0.7 copy.34
  166.0 0.7 copy.36.bg_ref
  166.7 0.7 copy.33
  167.4 0.7 copy.35
  168.1 20.3 %tail.1 = (bf16[64,64,384]{2,1,0:T(8,128)(2,1)}, bf16[4,32,64,128]{3,2,1,0:T(8,128)(2,1)}, bf16[3,32,64,128]{3,2,1,0:T(8,128)(2,1)}) custom-call(f32[64,384]{1,0:T(8,128)} %bitcast.32, bf16[16,64,1536]{2,1,0:T(8,128)(2,1)} %get-tuple-element.16.e1_ref, bf16[16,64,1536]{2,1,0:T(8,128)(2,1)} %get-tuple-element.17.g_ref, f32[16,1,1536]{2,1,0:T(1,128)} %reshape.28.m_ref, ...), custom_call_target="tpu_custom_call" | custom-call | tf_op jit(solution)/shard_map/tail/pallas_call | solution.py:480
  188.5 0.1 copy.37
  188.6 0.9 copy.38.w_ref
  189.4 0.5 bitcast_convert_fusion.bo_ref
  190.0 112.9 %outer_product.1 = bf16[48,384,128]{2,1,0:T(8,128)(2,1)} custom-call(bf16[4,32,64,128]{3,2,1,0:T(8,128)(2,1)} %get-tuple-element.19.a_ref, bf16[3,32,64,128]{3,2,1,0:T(8,128)(2,1)} %get-tuple-element.20.b_ref, bf16[48,384,128]{2,1,0:T(8,128)(2,1)} %z_ref.3, f32[48,1,384]{2,1,0:T(1,128)} %get-tuple-element.21.ninv_ref, bf16[128,1024]{1,0:T(8,128)(2,1)} %copy.38.w_ref, ...), custom_call_target="tpu_custom_call" | custom-call | tf_op jit(solution)/shard_map/outer_product/pallas_call | solution.py:497
  302.8 5.1 %copy.44 = bf16[48,384,128]{2,1,0:T(8,128)(2,1)} copy(bf16[48,384,128]{2,1,0:T(8,128)(2,1)} %outer_product.1) | data formatting | bytes 9437184
  (23 shorter events, 0.1 us)
Async XLA Ops:
  0.6 31.9 %slice-start = ((bf16[64,144]{1,0:T(8,128)(2,1)}), bf16[64,64]{1,0:T(8,128)(2,1)S(1)}, s32[]{:S(2)}) async-start(bf16[64,144]{1,0:T(8,128)(2,1)} %param.22), calls=%async_computation | async-start | bytes 32768 | tf_op jit(solution)/shard_map/slice | solution.py:442
  0.6 32.0 %copy-start.1 = (bf16[64,144]{1,0:T(8,128)(2,1)S(1)}, bf16[64,144]{1,0:T(8,128)(2,1)}, u32[]{:S(2)}) copy-start(bf16[64,144]{1,0:T(8,128)(2,1)} %param.22) | copy-start | bytes 55300
  0.7 32.8 %copy-start.2 = (bf16[64,256]{1,0:T(8,128)(2,1)S(1)}, bf16[64,256]{1,0:T(8,128)(2,1)}, u32[]{:S(2)}) copy-start(bf16[64,256]{1,0:T(8,128)(2,1)} %param.19) | copy-start | bytes 98308
  0.7 33.6 %copy-start.7 = (bf16[64]{0:T(256)(128)(2,1)S(1)}, bf16[64]{0:T(256)(128)(2,1)}, u32[]{:S(2)}) copy-start(bf16[64]{0:T(256)(128)(2,1)} %param.20) | copy-start | bytes 388
  0.7 34.3 %copy-start.4 = (bf16[64,64]{1,0:T(8,128)(2,1)S(1)}, bf16[64,64]{1,0:T(8,128)(2,1)}, u32[]{:S(2)}) copy-start(bf16[64,64]{1,0:T(8,128)(2,1)} %param.21) | copy-start | bytes 24580
  35.6 129.7 %copy-start.3 = (bf16[64,256]{1,0:T(8,128)(2,1)S(1)}, bf16[64,256]{1,0:T(8,128)(2,1)}, u32[]{:S(2)}) copy-start(bf16[64,256]{1,0:T(8,128)(2,1)} %param.25) | copy-start | bytes 98308
  35.6 130.4 %copy-start.8 = (bf16[64]{0:T(256)(128)(2,1)S(1)}, bf16[64]{0:T(256)(128)(2,1)}, u32[]{:S(2)}) copy-start(bf16[64]{0:T(256)(128)(2,1)} %param.23) | copy-start | bytes 388
  35.6 131.1 %copy-start.5 = (bf16[64,64]{1,0:T(8,128)(2,1)S(1)}, bf16[64,64]{1,0:T(8,128)(2,1)}, u32[]{:S(2)}) copy-start(bf16[64,64]{1,0:T(8,128)(2,1)} %param.24) | copy-start | bytes 24580
  35.6 131.8 %copy-start.6 = (bf16[64,64]{1,0:T(8,128)(2,1)S(1)}, bf16[64,64]{1,0:T(8,128)(2,1)}, u32[]{:S(2)}) copy-start(bf16[64,64]{1,0:T(8,128)(2,1)} %param.27) | copy-start | bytes 24580
  168.1 20.3 %copy-start = (bf16[32,32,128]{2,1,0:T(8,128)(2,1)S(1)}, bf16[32,32,128]{2,1,0:T(8,128)(2,1)}, u32[]{:S(2)}) copy-start(bf16[32,32,128]{2,1,0:T(8,128)(2,1)} %param.28) | copy-start | bytes 786436
  168.1 21.3 %copy-start.9 = (bf16[128]{0:T(256)(128)(2,1)S(1)}, bf16[128]{0:T(256)(128)(2,1)}, u32[]{:S(2)}) copy-start(bf16[128]{0:T(256)(128)(2,1)} %param.29) | copy-start | bytes 772

commit v3 on v1

v3 whole, which is shorter than its diff:
```python
import functools
import math

import jax
import jax.numpy as jnp
from jax import lax
from jax.experimental import pallas as pl
from jax.experimental.pallas import tpu as pltpu
from jax.sharding import PartitionSpec as P

MASK_FILL = -1e9
LOG2E = math.log2(math.e)
F32 = jnp.float32
BF16 = jnp.bfloat16
VMEM_LIMIT = 62 * 1024 * 1024
MESH = pl.DeviceIdType.MESH
SEQS = 4


def norm_rows(x):
    c = x - jnp.mean(x, axis=0, keepdims=True)
    var = jnp.mean(c * c, axis=0, keepdims=True)
    return (c * lax.rsqrt(var + 1e-5)).astype(BF16)


def dot(a, b):
    return jnp.dot(a, b, preferred_element_type=F32)


def dot_t(a, b):
    return lax.dot_general(a, b, (((1,), (1,)), ((), ())), preferred_element_type=F32)


def sigmoid(x):
    return 1.0 / (1.0 + jnp.exp(-x))


def wide_max(x):
    return jnp.max(jnp.max(x, axis=0, keepdims=True), axis=1, keepdims=True)[0, 0]


def enter(axis, me, n):
    barrier = pltpu.get_barrier_semaphore()
    for t in range(1, n):
        pl.semaphore_signal(barrier, inc=1, device_id={axis: lax.rem(me + t, n)}, device_id_type=MESH)
    pl.semaphore_wait(barrier, n - 1)


def neighbours(me, n):
    return lax.rem(me + 2, n), lax.rem(me + n - 2, n), lax.rem(me + 4, n), me + 1 - 2 * lax.rem(me, 2)


def remote(axis, sems, src, dst, to):
    return pltpu.make_async_remote_copy(src_ref=src, dst_ref=dst, send_sem=sems[0], recv_sem=sems[1],
                                        device_id={axis: to}, device_id_type=MESH)


class Gather:
    def __init__(self, axis, me, n, sems, own, view):
        right, left, far, other = neighbours(me, n)
        plan = [(own, view(me), right), (own, view(me), left), (own, view(me), other),
                (view(left, 0), view(left, 0), right), (view(right, 1), view(right, 1), left),
                (view(left), view(left), other), (view(right), view(right), other),
                (view(far, 0), view(far, 0), other), (view(far, 1), view(far, 1), other)]
        self.copy = lambda k: remote(axis, sems(k), *plan[k])

    def after(self, waits, starts):
        for k in waits:
            self.copy(k).wait_recv()
        for k in starts:
            self.copy(k).start()

    def open(self):
        self.after((), (0, 1, 2))

    def hand_on(self):
        self.after((0,), (3, 5))
        self.after((1,), (4, 6))

    def close(self):
        self.after((3,), (7,))
        self.after((4,), (8,))
        self.after((2, 5, 6, 7, 8), ())
        for k in range(9):
            self.copy(k).wait_send()


def identity(size):
    return (lax.broadcasted_iota(jnp.int32, (size, size), 0) == lax.broadcasted_iota(jnp.int32, (size, size), 1)).astype(BF16)


def flip(x):
    return jnp.transpose(x.astype(F32)).astype(BF16)


def column(row):
    k = row.shape[1]
    on = lax.broadcasted_iota(jnp.int32, (k, k), 0) == lax.broadcasted_iota(jnp.int32, (k, k), 1)
    return jnp.sum(jnp.where(on, jnp.broadcast_to(row.astype(F32), (k, k)), 0.0), axis=1, keepdims=True)


def mask_row(m_ref, first, count):
    return jnp.concatenate([m_ref[pl.ds(first + u, 1), :] for u in range(count)], axis=1).astype(F32)


def bias_kernel(axis, n, z_hbm, w_ref, m_ref, out_ref, mask_ref, ninv_ref, cnt_ref, z_ref, blk_ref, local, send_sem, recv_sem):
    rows, res, pd = z_ref.shape
    heads = w_ref.shape[0]
    nblk, tall = out_ref.shape[1], out_ref.shape[3]
    ns = m_ref.shape[0]
    step = 4
    me = lax.axis_index(axis)

    def fetch(ib):
        at = pl.ds(ib * tall, tall)
        return pltpu.make_async_copy(z_hbm.at[at], z_ref.at[at], local.at[ib])

    for ib in range(nblk):
        fetch(ib).start()
    mask_ref[me] = m_ref[...].astype(BF16)
    enter(axis, me, n)
    hh, hs = heads // 2, ns // 2
    sems = lambda t: lambda k: (send_sem.at[t, k], recv_sem.at[t, k])
    mask_ring = Gather(axis, me, n, sems(nblk), mask_ref.at[me],
                       lambda d, p=None: mask_ref.at[d] if p is None else mask_ref.at[d, pl.ds(p * hs, hs)])

    def ring(ib):
        return Gather(axis, me, n, sems(ib), out_ref.at[me, ib],
                      lambda d, p=None: out_ref.at[d, ib] if p is None else out_ref.at[d, ib, pl.ds(p * hh, hh)])

    mask_ring.open()
    eye = identity(pd)

    def block(ib, _):
        fetch(ib).wait()
        for t in range(tall // step):
            zt = dot_t(eye, z_ref[pl.ds(ib * tall + t * step, step)].reshape(step * res, pd))
            b = dot(w_ref[...], norm_rows(zt))
            for u in range(step):
                blk_ref[:, t * step + u, :] = b[:, u * res:(u + 1) * res]
        out_ref[me, ib] = blk_ref[...].astype(BF16)
        ring(ib).open()
        return 0

    lax.fori_loop(0, nblk, block, 0)
    mask_ring.hand_on()
    for ib in range(nblk):
        ring(ib).hand_on()
    mask_ring.close()
    mask = mask_ref[...].reshape(n * ns, res)
    pick = (lax.broadcasted_iota(jnp.int32, (rows, res), 1) ==
            lax.broadcasted_iota(jnp.int32, (rows, res), 0) + me * rows).astype(BF16)
    pairs = dot(dot_t(pick, mask).astype(BF16), mask)
    ninv = 1.0 / (pairs + 1e-3)
    for i in range(rows):
        ninv_ref[i] = ninv[i:i + 1]
    cnt_ref[...] = dot(jnp.ones((8, n * ns), BF16), mask)[0:1]
    for ib in range(nblk):
        ring(ib).close()


def row_kernel(heads, hd, scale, e_ref, m_ref, packed_ref, win_ref, bg_ref, wout_ref, cin_ref,
               e1_ref, g_ref, kv_ref, qsum_ref,
               rhs_ref, kaug_ref, va_ref, att_ref, bias_ref, wt_ref, ot_ref, ct_ref, gb_ref, top_ref):
    us, ch, res = e_ref.shape
    ht = heads * hd
    wide = us * res
    step = pl.program_id(0)

    @pl.when(step == 0)
    def _():
        rows = lax.broadcasted_iota(jnp.int32, rhs_ref.shape, 1)
        rhs_ref[...] = jnp.where(rows == 2 * ht, 1.0, 0.0).astype(BF16)
        qsum_ref[...] = jnp.zeros_like(qsum_ref)
        wt_ref[...] = flip(win_ref[...])
        ot_ref[...] = flip(wout_ref[...])
        ct = flip(cin_ref[...])
        r = lax.broadcasted_iota(jnp.int32, (ht, ht), 0)
        turn = (lax.broadcasted_iota(jnp.int32, (ht, ht), 1) == lax.rem(r, heads) * hd + r // heads).astype(BF16)
        ct_ref[...] = jnp.concatenate([dot(turn, ct[:ht]).astype(BF16), ct[ht:]], axis=0)
        gb_ref[...] = column(bg_ref[...])
        for h in range(heads):
            one = jnp.concatenate([packed_ref[d, t, h] for d in range(packed_ref.shape[0])
                                   for t in range(packed_ref.shape[1])], axis=0)
            bias_ref[h // 2, :, (h % 2) * res:(h % 2 + 1) * res] = jnp.transpose(one.astype(F32)) * LOG2E
        top = jnp.abs(bias_ref[0])
        for pr in range(1, heads // 2):
            top = jnp.maximum(top, jnp.abs(bias_ref[pr]))
        top_ref[0] = wide_max(top)

    x = jnp.concatenate([e_ref[u] for u in range(us)], axis=1).astype(F32)
    proj = dot(wt_ref[...], norm_rows(x)).astype(BF16).astype(F32)
    q, k, v, g = (proj[n * ht:(n + 1) * ht] for n in range(4))
    keep = mask_row(m_ref, step * us, us)
    qs = q * (scale * LOG2E)
    q_top = wide_max(jnp.sum((qs * qs).reshape(heads, hd, wide), axis=1))
    k_top = wide_max(jnp.sum((k * k).reshape(heads, hd, wide), axis=1))
    small = (q_top * k_top < 900.0) & (top_ref[0] < 30.0)

    first_half = (lax.broadcasted_iota(jnp.int32, (ht, wide), 0) % 16) < 8
    hi = qs.astype(BF16).astype(F32)
    for n, part in enumerate((hi, qs - hi)):
        even = jnp.where(first_half, part, 0.0).astype(BF16)
        odd = jnp.where(first_half, 0.0, part).astype(BF16)
        for u in range(us):
            for h in range(heads):
                rows = slice(16 * (h // 2), 16 * (h // 2) + 16)
                rhs_ref[u, n * ht + rows.start:n * ht + rows.stop, h * res:(h + 1) * res] = \
                    (odd if h % 2 else even)[rows, u * res:(u + 1) * res]
    pen = jnp.where(lax.broadcasted_iota(jnp.int32, (16, wide), 0) == 0,
                    jnp.broadcast_to(jnp.where(keep > 0, 0.0, -1e30), (16, wide)), 0.0)
    kaug_ref[...] = jnp.transpose(jnp.concatenate([k, k, pen], axis=0)).astype(BF16)
    ones = jnp.where(lax.broadcasted_iota(jnp.int32, (8, wide), 0) == 0, 1.0, 0.0)
    for pr in range(heads // 2):
        va_ref[pr] = jnp.concatenate([v[16 * pr:16 * pr + 8], ones, v[16 * pr + 8:16 * pr + 16], ones], axis=0).astype(BF16)

    @pl.when(small)
    def _():
        for u in range(us):
            cols = slice(u * res, (u + 1) * res)
            for pr in range(heads // 2):
                s = dot(kaug_ref[cols], rhs_ref[u, :, 2 * pr * res:(2 * pr + 2) * res]) + bias_ref[pr]
                o = dot(va_ref[pr, :, cols], jnp.exp2(s).astype(BF16))
                att_ref[16 * pr:16 * pr + 8, cols] = o[0:8, :res] / o[8:9, :res]
                att_ref[16 * pr + 8:16 * pr + 16, cols] = o[16:24, res:] / o[24:25, res:]
            some = jnp.max(keep[:, cols], axis=1, keepdims=True) > 0
            flat = jnp.mean(v[:, cols], axis=1, keepdims=True)
            att_ref[:, cols] = jnp.where(some, att_ref[:, cols], flat)

    @pl.when(jnp.logical_not(small))
    def _():
        def one(t, _):
            u, pr = t // (heads // 2), t % (heads // 2)
            cols = pl.ds(pl.multiple_of(u * res, res), res)
            s = dot(kaug_ref[cols], rhs_ref[u, :, pl.ds(pl.multiple_of(2 * pr * res, 2 * res), 2 * res)]) + bias_ref[pr]
            p = jnp.exp2(s - jnp.max(s, axis=0, keepdims=True)).astype(BF16)
            o = dot(va_ref[pr, :, cols], p)
            att_ref[pl.ds(pl.multiple_of(16 * pr, 16), 8), cols] = o[0:8, :res] / o[8:9, :res]
            att_ref[pl.ds(pl.multiple_of(16 * pr + 8, 8), 8), cols] = o[16:24, res:] / o[24:25, res:]
            return 0

        lax.fori_loop(0, us * (heads // 2), one, 0)

    gated = (sigmoid(g + gb_ref[...]) * att_ref[...]).astype(BF16)
    e1 = (x + dot(ot_ref[...], gated)).astype(BF16)
    e1_ref[0] = e1
    col = dot(ct_ref[...], norm_rows(e1.astype(F32))).astype(BF16)
    part = col[:ht].astype(F32) * keep
    tot = part[:, :res]
    for u in range(1, us):
        tot = tot + part[:, u * res:(u + 1) * res]
    qsum_ref[...] += tot
    g_ref[0] = col[ht:2 * ht]
    kv_ref[0] = col[2 * ht:]


def exchange(axis, me, n, srcs, dst, send_sem, recv_sem):
    copies = []
    for t in range(1, n):
        peer = lax.rem(me + t, n)
        copy = pltpu.make_async_remote_copy(src_ref=srcs(peer), dst_ref=dst.at[me], send_sem=send_sem.at[t],
                                            recv_sem=recv_sem.at[t], device_id={axis: peer}, device_id_type=MESH)
        copy.start()
        copies.append(copy)
    return copies


def col_kernel(axis, n, heads, hd, scale, qsum_ref, cnt_ref, kv_ref, m_ref, o_ref,
               l_ref, qp_ref, qb_ref, st_ref, sp_ref, send_sem, recv_sem):
    ng, _, wide = kv_ref.shape
    res = qsum_ref.shape[1]
    us = wide // res
    ht = heads * hd
    me = lax.axis_index(axis)
    enter(axis, me, n)
    blk = ht // n
    mine = pl.ds(pl.multiple_of(me * blk, blk), blk)
    copies = exchange(axis, me, n, lambda p: qsum_ref.at[pl.ds(pl.multiple_of(p * blk, blk), blk)], qp_ref,
                      send_sem.at[0], recv_sem.at[0])
    qp_ref[me] = qsum_ref[mine]
    for c in copies:
        c.wait()
    tot = qp_ref[0]
    for t in range(1, n):
        tot = tot + qp_ref[t]
    qb_ref[me] = (tot / (cnt_ref[...] + 1e-10)).astype(BF16).astype(F32)
    copies = exchange(axis, me, n, lambda p: qb_ref.at[me], qb_ref, send_sem.at[1], recv_sem.at[1])
    for c in copies:
        c.wait()
    qbar = qb_ref[...].reshape(ht, res)

    def logits(gr, top):
        for u in range(us):
            cols = slice(u * res, (u + 1) * res)
            kv = kv_ref[gr, :, cols].astype(F32)
            acc = qbar[0:heads] * kv[0:1]
            for d in range(1, hd):
                acc = acc + qbar[d * heads:(d + 1) * heads] * kv[d:d + 1]
            acc = jnp.where(m_ref[pl.ds(gr * us + u, 1), :] > 0, acc * scale, MASK_FILL)
            l_ref[gr, :, cols] = acc
            top = jnp.maximum(top, acc)
        return top

    top = lax.fori_loop(0, ng, logits, jnp.full((heads, res), -3e38, F32))

    def sums(gr, carry):
        for u in range(us):
            cols = slice(u * res, (u + 1) * res)
            w = jnp.exp(l_ref[gr, :, cols] - top)
            kv = kv_ref[gr, :, cols].astype(F32)
            carry = (carry[0] + w,) + tuple(carry[1 + d] + w * kv[hd + d:hd + d + 1] for d in range(hd))
        return carry

    zero = jnp.zeros((heads, res), F32)
    tot = lax.fori_loop(0, ng, sums, (zero,) * (hd + 1))
    for d in range(hd):
        st_ref[:, d, :] = tot[1 + d]
    st_ref[:, hd, :] = tot[0]
    st_ref[:, hd + 1, :] = top
    for d in range(hd + 2, st_ref.shape[1]):
        st_ref[:, d, :] = zero
    copies = exchange(axis, me, n, lambda p: st_ref.at[p], sp_ref, send_sem.at[2], recv_sem.at[2])
    sp_ref[me] = st_ref[me]
    for c in copies:
        c.wait()
    best = sp_ref[0, hd + 1:hd + 2]
    for t in range(1, n):
        best = jnp.maximum(best, sp_ref[t, hd + 1:hd + 2])
    num = jnp.zeros((hd, res), F32)
    den = jnp.zeros((1, res), F32)
    for t in range(n):
        fac = jnp.exp(sp_ref[t, hd + 1:hd + 2] - best)
        num = num + sp_ref[t, 0:hd] * fac
        den = den + sp_ref[t, hd:hd + 1] * fac
    o_ref[me] = num / den
    copies = exchange(axis, me, n, lambda p: o_ref.at[me], o_ref, send_sem.at[3], recv_sem.at[3])
    for c in copies:
        c.wait()


def tail_kernel(axis, n, o_ref, e1_hbm, g_hbm, m_ref, bg_ref, wout_ref, tin_ref, tout_ref, opm_ref,
                z_hbm, ninv_ref, w_ref, bo_ref, e3_hbm, out_hbm,
                e1_ref, g_ref, e3_ref, z_ref, buf_ref, a_ref, b_ref, ag_ref, tr_ref, bg_all, at_ref, hi_ref, lo_ref,
                wp_ref, wf_ref, local, asend, arecv, bsend, brecv):
    rows, res, pd = z_ref.shape
    nb, odim, ns, jb = b_ref.shape
    chips = a_ref.shape[0]
    ht = o_ref.shape[0]
    wide = e1_ref.shape[2]
    us = wide // res
    tb = buf_ref.shape[1]
    ngr = ns // tb
    per = tb // us
    ib = 2 * hi_ref.shape[0]
    half = odim // 2
    me = lax.axis_index(axis)
    chip, core = me // 2, lax.rem(me, 2)
    right, left, far, other = neighbours(me, n)
    up, down, across = lax.rem(chip + 1, chips), lax.rem(chip + chips - 1, chips), lax.rem(chip + 2, chips)

    def fetch(g):
        at = pl.ds(g * per, per)
        return [pltpu.make_async_copy(e1_hbm.at[at], e1_ref.at[at], local.at[0, g]),
                pltpu.make_async_copy(g_hbm.at[at], g_ref.at[at], local.at[1, g])]

    for g in range(ngr):
        for c in fetch(g):
            c.start()
    z_in = pltpu.make_async_copy(z_hbm, z_ref, local.at[2, 0])
    z_in.start()
    enter(axis, me, n)

    part = {None: slice(None), 0: pl.ds(0, half), 1: pl.ds(half, half)}

    def a_copies(g):
        seqs = pl.ds(pl.multiple_of(g * tb, tb), tb)
        src = lambda c, p=None: a_ref.at[c, part[p], seqs]
        dst = lambda d, p=None: ag_ref.at[d, part[p], seqs]
        tr = lambda t: tr_ref.at[t, :, seqs]
        plan = [(src(across, 0), tr(0), right), (src(across, 1), tr(1), left), (src(up), dst(me), right),
                (src(down), dst(me), left), (src(chip), dst(me), other),
                (tr(0), dst(left, 0), right), (tr(1), dst(right, 1), left),
                (dst(left), dst(left), other), (dst(right), dst(right), other),
                (dst(far, 0), dst(far, 0), other), (dst(far, 1), dst(far, 1), other)]
        return lambda k: remote(axis, (asend.at[g, k], arecv.at[g, k]), *plan[k])

    def b_first(g):
        seqs = pl.ds(pl.multiple_of(g * tb, tb), tb)
        return Gather(axis, me, n, lambda k: (bsend.at[g, k], brecv.at[g, k]), b_ref.at[0, :, seqs],
                      lambda d, p=None: bg_all.at[0, d, part[p], seqs])

    def b_rest(t):
        return Gather(axis, me, n, lambda k: (bsend.at[ngr - 1 + t, k], brecv.at[ngr - 1 + t, k]), b_ref.at[t],
                      lambda d, p=None: bg_all.at[t, d] if p is None else bg_all.at[t, d, part[p]])

    src = lax.broadcasted_iota(jnp.int32, (res, chips * jb), 0)
    dst = lax.broadcasted_iota(jnp.int32, (res, chips * jb), 1)
    hj = jb // 2
    place = ((dst % hj < rows) & (src == (dst // hj) * rows + dst % hj)).astype(BF16)

    wout, tin, opm = (flip(r[...]) for r in (wout_ref, tin_ref, opm_ref))
    gate_bias = column(bg_ref[...])

    def group(g, _):
        seqs = pl.ds(pl.multiple_of(g * tb, tb), tb)
        for c in fetch(g):
            c.wait()
        o = jnp.concatenate([o_ref[...]] * us, axis=1)
        for j in range(per):
            gr = g * per + j
            gated = (sigmoid(g_ref[gr].astype(F32) + gate_bias) * o).astype(BF16)
            e2 = (e1_ref[gr].astype(F32) + dot(wout, gated)).astype(BF16).astype(F32)
            hid = jnp.maximum(dot(tin, norm_rows(e2)), 0.0).astype(BF16)
            e3 = (e2 + dot(tout_ref[...], hid)).astype(BF16)
            ab = dot(opm, norm_rows(e3.astype(F32))).astype(BF16).astype(F32) * mask_row(m_ref, gr * us, us)
            for u in range(us):
                cols = slice(u * res, (u + 1) * res)
                e3_ref[gr * us + u] = e3[:, cols]
                buf_ref[:, j * us + u, :] = ab[:, cols]
        moved = dot(buf_ref[0:odim].astype(BF16).reshape(odim * tb, res), place).astype(BF16)
        for c in range(chips):
            a_ref[c, :, seqs, :] = moved[:, c * jb:(c + 1) * jb].reshape(odim, tb, jb)
        for t in range(nb):
            blk = buf_ref[odim:, :, t * jb:(t + 1) * jb].astype(BF16)
            b_ref[t, :, seqs, :] = blk
            bg_all[t, me, :, seqs, :] = blk
        ac = a_copies(g)
        for k in range(5):
            ac(k).start()
        b_first(g).open()
        ag_ref[me, :, seqs, :] = a_ref[chip, :, seqs, :]
        return 0

    lax.fori_loop(0, ngr, group, 0)
    e3_out = pltpu.make_async_copy(e3_ref, e3_hbm, local.at[2, 1])
    e3_out.start()

    def pass_on(g, _):
        ac = a_copies(g)
        for wait, start in ((0, 5), (1, 6), (2, 7), (3, 8)):
            ac(wait).wait_recv()
            ac(start).start()
        b_first(g).hand_on()
        return 0

    lax.fori_loop(0, ngr, pass_on, 0)
    b_rest(1).open()

    def finish_a(g, _):
        ac = a_copies(g)
        for wait, start in ((5, 9), (6, 10)):
            ac(wait).wait_recv()
            ac(start).start()
        for k in (4, 7, 8, 9, 10):
            ac(k).wait_recv()
        for k in range(11):
            ac(k).wait_send()
        return 0

    lax.fori_loop(0, ngr, finish_a, 0)
    wf_ref[...] = w_ref[...].astype(F32)
    for d in range(odim):
        wp_ref[:, d * odim:(d + 1) * odim] = jnp.transpose(wf_ref[:, d, :]).astype(BF16)
    pick = (lax.broadcasted_iota(jnp.int32, (rows, jb), 1) ==
            lax.broadcasted_iota(jnp.int32, (rows, jb), 0) + core * hj).astype(BF16)
    for c in range(odim):
        at_ref[:, c, :] = dot_t(pick, ag_ref[:, c].reshape(n * ns, jb))

    def finish_b(g, _):
        b_first(g).close()
        return 0

    lax.fori_loop(0, ngr, finish_b, 0)
    z_in.wait()
    steps = rows // ib

    def done(t):
        at = pl.ds(t * jb, jb)
        return pltpu.make_async_copy(z_ref.at[:, at], out_hbm.at[:, at], local.at[3, t])

    def body(k, _):
        t = k // steps
        base = lax.rem(k, steps) * ib
        cols = pl.ds(pl.multiple_of(t * jb, jb), jb)

        for later in range(1, nb):
            @pl.when(k == (later - 1) * steps + steps // 2)
            def _():
                b_rest(later).hand_on()
                if later + 1 < nb:
                    b_rest(later + 1).open()

            @pl.when(k == later * steps)
            def _():
                b_rest(later).close()
                done(later - 1).start()

        a = at_ref[pl.ds(base, ib)].reshape(ib * odim, n * ns).astype(BF16)
        for q in range(odim // 2):
            rhs = jnp.concatenate([bg_all[t, :, 2 * q].reshape(n * ns, jb), bg_all[t, :, 2 * q + 1].reshape(n * ns, jb)], axis=1)
            pr = dot(a, rhs)
            hi = pr.astype(BF16)
            lo = (pr - hi.astype(F32)).astype(BF16)
            for val, ref in ((hi, hi_ref), (lo, lo_ref)):
                for i in range(ib):
                    for h in range(2):
                        ref[i // 2, (2 * q + h) * odim:(2 * q + h + 1) * odim, (i % 2) * jb:(i % 2 + 1) * jb] = \
                            val[i * odim:(i + 1) * odim, h * jb:(h + 1) * jb]
        for ip in range(ib // 2):
            zt = dot(wp_ref[...], hi_ref[ip]) + dot(wp_ref[...], lo_ref[ip])
            for h in range(2):
                i = base + 2 * ip + h
                upd = jnp.transpose(zt[:, h * jb:(h + 1) * jb] * ninv_ref[i, :, cols])
                z_ref[i, cols, :] = (z_ref[i, cols, :].astype(F32) + upd + bo_ref[...].astype(F32)).astype(BF16)
        return 0

    lax.fori_loop(0, nb * steps, body, 0)
    done(nb - 1).start()
    for t in range(nb):
        done(t).wait()
    e3_out.wait()


def solution(mesh):
    row_spec = P(('batch', 'seq'))
    rep_spec = P()
    n_seq = mesh.shape['seq']

    def local_block(msa, mask, pair, w_pair_bias, w_row_in, b_row_gate, w_row_out, w_col_in, b_col_gate, w_col_out,
                    w_trans_in, w_trans_out, w_opm_in, w_opm_out, b_opm_out):
        ns, res, ch = msa.shape
        rows = pair.shape[0]
        pd = pair.shape[-1]
        heads = w_pair_bias.shape[1]
        ht = w_row_out.shape[0]
        hd = ht // heads
        odim = w_opm_out.shape[0]
        scale = hd ** -0.5
        params = functools.partial(pltpu.CompilerParams, vmem_limit_bytes=VMEM_LIMIT)

        vm = pl.BlockSpec(memory_space=pltpu.VMEM)
        hbm = pl.BlockSpec(memory_space=pl.ANY)
        dma = pltpu.SemaphoreType.DMA
        tall = 16
        nblk = rows // tall
        packed, _, ninv, counts = pl.pallas_call(
            functools.partial(bias_kernel, 'seq', n_seq),
            in_specs=[hbm, vm, vm],
            out_specs=[vm] * 4,
            out_shape=[jax.ShapeDtypeStruct((n_seq, nblk, heads, tall, res), BF16), jax.ShapeDtypeStruct((n_seq, ns, res), BF16),
                       jax.ShapeDtypeStruct((rows, 1, res), F32), jax.ShapeDtypeStruct((1, res), F32)],
            scratch_shapes=[pltpu.VMEM((rows, res, pd), BF16), pltpu.VMEM((heads, tall, res), F32), dma((nblk,)),
                            dma((nblk + 1, 9)), dma((nblk + 1, 9))],
            compiler_params=params(collective_id=1, has_side_effects=True),
            name='pair_bias',
        )(pair, w_pair_bias.T, mask)

        us = SEQS
        ng, wide = ns // us, us * res
        ncol = w_col_in.shape[1]

        full = lambda *shape: pl.BlockSpec(shape, lambda *g: (0,) * len(shape))
        group = lambda k, r: pl.BlockSpec((k, r, wide), lambda s: (s, 0, 0))
        e1, gate, kv, qsum = pl.pallas_call(
            functools.partial(row_kernel, heads, hd, scale),
            grid=(ng,),
            in_specs=[pl.BlockSpec((us, ch, res), lambda s: (s, 0, 0)), full(ns, res),
                      full(n_seq, nblk, heads, tall, res), full(ch, 4 * ht), full(1, ht), full(ht, ch), full(ch, ncol)],
            out_specs=[group(1, ch), group(1, ht), group(1, 2 * hd), full(ht, res)],
            out_shape=[jax.ShapeDtypeStruct((ng, ch, wide), BF16), jax.ShapeDtypeStruct((ng, ht, wide), BF16),
                       jax.ShapeDtypeStruct((ng, 2 * hd, wide), BF16), jax.ShapeDtypeStruct((ht, res), F32)],
            scratch_shapes=[pltpu.VMEM((us, 2 * ht + 16, heads * res), BF16), pltpu.VMEM((wide, 2 * ht + 16), BF16),
                            pltpu.VMEM((heads // 2, 32, wide), BF16), pltpu.VMEM((ht, wide), F32),
                            pltpu.VMEM((heads // 2, res, 2 * res), F32), pltpu.VMEM((4 * ht, ch), BF16),
                            pltpu.VMEM((ch, ht), BF16), pltpu.VMEM((ncol, ch), BF16), pltpu.VMEM((ht, 1), F32), pltpu.SMEM((1,), F32)],
            compiler_params=params(dimension_semantics=('arbitrary',)),
            name='row_attention',
        )(jnp.transpose(msa, (0, 2, 1)), mask, packed, w_row_in, b_row_gate.reshape(1, ht), w_row_out, w_col_in)

        col_o = pl.pallas_call(
            functools.partial(col_kernel, 'seq', n_seq, heads, hd, scale),
            in_specs=[pl.BlockSpec(memory_space=pltpu.VMEM)] * 4,
            out_specs=pl.BlockSpec(memory_space=pltpu.VMEM),
            out_shape=jax.ShapeDtypeStruct((heads, hd, res), F32),
            scratch_shapes=[pltpu.VMEM((ng, heads, wide), F32), pltpu.VMEM((n_seq, ht // n_seq, res), F32),
                            pltpu.VMEM((n_seq, ht // n_seq, res), F32), pltpu.VMEM((heads, 16, res), F32),
                            pltpu.VMEM((n_seq, 16, res), F32), pltpu.SemaphoreType.DMA((4, n_seq)),
                            pltpu.SemaphoreType.DMA((4, n_seq))],
            compiler_params=params(collective_id=0, has_side_effects=True),
            name='col_stats',
        )(qsum, counts, kv, mask).reshape(ht, res)

        tb, jb, ib = 16, 128, 8
        chips = n_seq // 2
        nb = res // jb
        e3, pair_out = pl.pallas_call(
            functools.partial(tail_kernel, 'seq', n_seq),
            in_specs=[vm, hbm, hbm] + [vm] * 6 + [hbm] + [vm] * 3,
            out_specs=[hbm, hbm],
            out_shape=[jax.ShapeDtypeStruct((ns, ch, res), BF16), jax.ShapeDtypeStruct((rows, res, pd), BF16)],
            scratch_shapes=[pltpu.VMEM((ng, ch, wide), BF16), pltpu.VMEM((ng, ht, wide), BF16), pltpu.VMEM((ns, ch, res), BF16),
                            pltpu.VMEM((rows, res, pd), BF16), pltpu.VMEM((2 * odim, tb, res), F32),
                            pltpu.VMEM((chips, odim, ns, jb), BF16), pltpu.VMEM((nb, odim, ns, jb), BF16),
                            pltpu.VMEM((n_seq, odim, ns, jb), BF16), pltpu.VMEM((2, odim // 2, ns, jb), BF16),
                            pltpu.VMEM((nb, n_seq, odim, ns, jb), BF16), pltpu.VMEM((rows, odim, n_seq * ns), F32),
                            pltpu.VMEM((ib // 2, odim * odim, 2 * jb), BF16), pltpu.VMEM((ib // 2, odim * odim, 2 * jb), BF16),
                            pltpu.VMEM((pd, odim * odim), BF16), pltpu.VMEM((odim, odim, pd), F32),
                            dma((4, max(4, ns // tb))), dma((ns // tb, 11)), dma((ns // tb, 11)),
                            dma((ns // tb + nb - 1, 9)), dma((ns // tb + nb - 1, 9))],
            compiler_params=params(collective_id=2, has_side_effects=True),
            name='tail_outer_product',
        )(col_o, e1, gate, mask, b_col_gate.reshape(1, ht), w_col_out, w_trans_in, w_trans_out.T, w_opm_in,
          pair, ninv, w_opm_out, b_opm_out.reshape(1, pd))
        return jnp.transpose(e3, (0, 2, 1)), pair_out

    return jax.shard_map(local_block, mesh=mesh, in_specs=(row_spec, row_spec, row_spec) + (rep_spec,) * 12,
                         out_specs=(row_spec, row_spec), check_vma=False)
```

time: 349 us -> 265 us (0.76)
  Pallas kernels: 193 us -> 258 us
  waiting for transfers between devices: 53.2 us -> 0 us
  local copies, waits for them, and re-layouts: 58.5 us -> 6.23 us
  other arithmetic: 15.7 us -> 0 us
  between operations: 14.4 us -> 0.66 us
  matrix products: 8.24 us -> 0 us
  starting transfers between devices: 4.91 us -> 0 us
    pallas_call x2, Pallas kernels: 61.6 us -> 129 us  [the longest x1 106 us: local_block(): pl.pallas_call(functools.partial(tail_kernel, 'seq', n_seq), in_specs=[vm...]
    all_to_all x1 -> x0, waiting for transfers between devices: 27.4 us -> none  [local_block(): lax.all_to_all(ab[:odim].reshape(odim, ns, n_seq, rows), 'seq', split_axi...]
    all_gather x2 -> x0, waiting for transfers between devices: 25.7 us -> none  [the longest x1 13.9 us: local_block(): packed = lax.all_gather(packed, 'seq', axis=0)]
    unnamed x40 -> x4, local copies, waits for them, and re-layouts: 25.1 us -> 6.23 us
    reduce_sum x3 -> x0, other arithmetic: 10.5 us -> none  [the longest x1 5.47 us: layer_norm(): variance = jnp.mean(centered * centered, axis=-1, keepdims=True)]
    another operation x2 -> x0, local copies, waits for them, and re-layouts: 10.3 us -> none  [local_block(): lax.all_to_all(ab[:odim].reshape(odim, ns, n_seq, rows), 'seq', split_axi...]
    mul x2 -> x0, local copies, waits for them, and re-layouts: 8.67 us -> none  [local_block(): jnp.transpose(bias_t, (0, 2, 1, 3)).reshape(heads // 2, res, 2 * res)]
    dot_general x2 -> x0, matrix products: 8.24 us -> none  [the longest x1 7.93 us: local_block(): jnp.einsum('ijc,ch->hij', layer_norm(pair), w_pair_bias, preferred_elemen...]
  transfers between devices with their start and end apart: 3 -> 0, of which waited for: 3 -> 0; matrix products, arithmetic and copies ran while one was open for 14% -> 0% of each run, Pallas kernels for 0% -> 0%
where the time goes in v3:
time: 265 us
  Pallas kernels  258 us (97%)
  local copies, waits for them, and re-layouts  6.23 us (2%)
    pallas_call x1, Pallas kernels, local_block(): pl.pallas_call(functools.partial(row_kernel, heads, hd, scale), grid=(ng,...  107 us
    pallas_call x1, Pallas kernels, local_block(): pl.pallas_call(functools.partial(tail_kernel, 'seq', n_seq), in_specs=[vm...  106 us
    pallas_call x1, Pallas kernels, local_block(): pl.pallas_call(functools.partial(bias_kernel, 'seq', n_seq), in_specs=[hb...  23.2 us
    pallas_call x1, Pallas kernels, local_block(): pl.pallas_call(functools.partial(col_kernel, 'seq', n_seq, heads, hd, sca...  22.2 us
    unnamed x4, local copies, waits for them, and re-layouts  6.23 us

profile of v3, /device:TPU:113, one launch (start us, length us, event | category | flops | bytes accessed | tf_op | source)
XLA Modules:
  0.0 264.9 jit_solution(1155623278289544333)
XLA Ops:
  0.6 23.2 %pair_bias.1 = (bf16[8,3,8,16,384]{4,3,2,1,0:T(8,128)(2,1)}, bf16[8,64,384]{2,1,0:T(8,128)(2,1)}, f32[48,1,384]{2,1,0:T(1,128)}, f32[1,384]{1,0:T(1,128)}) custom-call(bf16[48,384,128]{2,1,0:T(8,128)(2,1)} %z_hbm.3, bf16[8,128]{1,0:T(8,128)(2,1)} %bitcast.12, s32[64,384]{1,0:T(8,128)} %m_ref.7), custom_call_target="tpu_custom_call" | custom-call | tf_op jit(solution)/shard_map/pair_bias/pallas_call | solution.py:546
  23.9 106.9 %row_attention.1 = (bf16[16,64,1536]{2,1,0:T(8,128)(2,1)}, bf16[16,64,1536]{2,1,0:T(8,128)(2,1)}, bf16[16,16,1536]{2,1,0:T(8,128)(2,1)}, f32[64,384]{1,0:T(8,128)}) custom-call(bf16[64,64,384]{2,1,0:T(8,128)(2,1)} %bitcast.8, s32[64,384]{1,0:T(8,128)} %m_ref.7, bf16[8,3,8,16,384]{4,3,2,1,0:T(8,128)(2,1)} %get-tuple-element.11.packed_ref, ...), custom_call_target="tpu_custom_call" | custom-call | tf_op jit(solution)/shard_map/row_attention/pallas_call | solution.py:564
  130.8 22.2 %col_stats.1 = f32[8,8,384]{2,1,0:T(8,128)} custom-call(f32[64,384]{1,0:T(8,128)} %get-tuple-element.12.qsum_ref, f32[1,384]{1,0:T(1,128)} %get-tuple-element.13.cnt_ref, bf16[16,16,1536]{2,1,0:T(8,128)(2,1)} %get-tuple-element.14.kv_ref, s32[64,384]{1,0:T(8,128)} %m_ref.7), custom_call_target="tpu_custom_call" | custom-call | tf_op jit(solution)/shard_map/col_stats/pallas_call | solution.py:580
  153.0 105.6 %tail_outer_product.1 = (bf16[64,64,384]{2,1,0:T(8,128)(2,1)}, bf16[48,384,128]{2,1,0:T(8,128)(2,1)}) custom-call(f32[64,384]{1,0:T(8,128)} %bitcast.10, bf16[16,64,1536]{2,1,0:T(8,128)(2,1)} %get-tuple-element.15.e1_hbm, bf16[16,64,1536]{2,1,0:T(8,128)(2,1)} %get-tuple-element.16.g_hbm, s32[64,384]{1,0:T(8,128)} %m_ref.7, bf16[1,64]{1,0:T(2,128)(2,1)} %bitcast.14, ...), custom_call_target="tpu_custom_call" | custom-call | tf_op jit(solution)/shard_map/tail_outer_product/pallas_call | solution.py:596
  258.6 0.0 copy-start
  258.6 4.0 %copy.19 = bf16[64,384,64]{1,2,0:T(8,128)(2,1)} copy(bf16[64,384,64]{1,2,0:T(8,128)(2,1)} %bitcast.9) | data formatting | bytes 6291456
  262.7 0.0 copy-done
  262.7 2.2 copy.20
Async XLA Ops:
  258.6 4.0 %copy-start = (bf16[48,384,128]{2,1,0:T(8,128)(2,1)S(1)}, bf16[48,384,128]{2,1,0:T(8,128)(2,1)}, u32[]{:S(2)}) copy-start(bf16[48,384,128]{2,1,0:T(8,128)(2,1)} %get-tuple-element.23) | copy-start | bytes 14155780

commit v4 on v3

--- a/solution.py
+++ b/solution.py
@@ -14,7 +14,7 @@
 BF16 = jnp.bfloat16
 VMEM_LIMIT = 62 * 1024 * 1024
 MESH = pl.DeviceIdType.MESH
-SEQS = 4
+SEQS = 8
 
 
 def norm_rows(x):
@@ -161,7 +161,7 @@
 
 def row_kernel(heads, hd, scale, e_ref, m_ref, packed_ref, win_ref, bg_ref, wout_ref, cin_ref,
                e1_ref, g_ref, kv_ref, qsum_ref,
-               rhs_ref, kaug_ref, va_ref, att_ref, bias_ref, wt_ref, ot_ref, ct_ref, gb_ref, top_ref):
+               rhs_ref, kaug_ref, va_ref, att_ref, bias_ref, xn_ref, wt_ref, ot_ref, ct_ref, gb_ref, top_ref):
     us, ch, res = e_ref.shape
     ht = heads * hd
     wide = us * res
@@ -188,14 +188,22 @@
             top = jnp.maximum(top, jnp.abs(bias_ref[pr]))
         top_ref[0] = wide_max(top)
 
-    x = jnp.concatenate([e_ref[u] for u in range(us)], axis=1).astype(F32)
-    proj = dot(wt_ref[...], norm_rows(x)).astype(BF16).astype(F32)
-    q, k, v, g = (proj[n * ht:(n + 1) * ht] for n in range(4))
+    def source():
+        return jnp.concatenate([e_ref[u] for u in range(us)], axis=1).astype(F32)
+
+    def project(n):
+        return dot(wt_ref[n * ht:(n + 1) * ht], xn_ref[...]).astype(BF16)
+
+    xn_ref[...] = norm_rows(source())
     keep = mask_row(m_ref, step * us, us)
-    qs = q * (scale * LOG2E)
-    q_top = wide_max(jnp.sum((qs * qs).reshape(heads, hd, wide), axis=1))
-    k_top = wide_max(jnp.sum((k * k).reshape(heads, hd, wide), axis=1))
-    small = (q_top * k_top < 900.0) & (top_ref[0] < 30.0)
+    qs = project(0).astype(F32) * (scale * LOG2E)
+    k = project(1)
+    v = project(2).astype(F32)
+    per_head = (lax.broadcasted_iota(jnp.int32, (heads, ht), 1) // hd ==
+                lax.broadcasted_iota(jnp.int32, (heads, ht), 0)).astype(BF16)
+    q_top = wide_max(dot(per_head, (qs * qs).astype(BF16)))
+    k_top = wide_max(dot(per_head, k * k))
+    small = (q_top * k_top < 880.0) & (top_ref[0] < 30.0) & (wide_max(jnp.abs(v)) < 1e15)
 
     first_half = (lax.broadcasted_iota(jnp.int32, (ht, wide), 0) % 16) < 8
     hi = qs.astype(BF16).astype(F32)
@@ -209,7 +217,7 @@
                     (odd if h % 2 else even)[rows, u * res:(u + 1) * res]
     pen = jnp.where(lax.broadcasted_iota(jnp.int32, (16, wide), 0) == 0,
                     jnp.broadcast_to(jnp.where(keep > 0, 0.0, -1e30), (16, wide)), 0.0)
-    kaug_ref[...] = jnp.transpose(jnp.concatenate([k, k, pen], axis=0)).astype(BF16)
+    kaug_ref[...] = jnp.transpose(jnp.concatenate([k, k, pen.astype(BF16)], axis=0))
     ones = jnp.where(lax.broadcasted_iota(jnp.int32, (8, wide), 0) == 0, 1.0, 0.0)
     for pr in range(heads // 2):
         va_ref[pr] = jnp.concatenate([v[16 * pr:16 * pr + 8], ones, v[16 * pr + 8:16 * pr + 16], ones], axis=0).astype(BF16)
@@ -241,8 +249,8 @@
 
         lax.fori_loop(0, us * (heads // 2), one, 0)
 
-    gated = (sigmoid(g + gb_ref[...]) * att_ref[...]).astype(BF16)
-    e1 = (x + dot(ot_ref[...], gated)).astype(BF16)
+    gated = (sigmoid(project(3).astype(F32) + gb_ref[...]) * att_ref[...]).astype(BF16)
+    e1 = (source() + dot(ot_ref[...], gated)).astype(BF16)
     e1_ref[0] = e1
     col = dot(ct_ref[...], norm_rows(e1.astype(F32))).astype(BF16)
     part = col[:ht].astype(F32) * keep
@@ -265,14 +273,13 @@
     return copies
 
 
-def col_kernel(axis, n, heads, hd, scale, qsum_ref, cnt_ref, kv_ref, m_ref, o_ref,
-               l_ref, qp_ref, qb_ref, st_ref, sp_ref, send_sem, recv_sem):
+def column_attention(axis, n, heads, hd, scale, qsum_ref, cnt_ref, kv_ref, m_ref, o_ref,
+                     l_ref, qp_ref, qb_ref, st_ref, sp_ref, send_sem, recv_sem):
     ng, _, wide = kv_ref.shape
     res = qsum_ref.shape[1]
     us = wide // res
     ht = heads * hd
     me = lax.axis_index(axis)
-    enter(axis, me, n)
     blk = ht // n
     mine = pl.ds(pl.multiple_of(me * blk, blk), blk)
     copies = exchange(axis, me, n, lambda p: qsum_ref.at[pl.ds(pl.multiple_of(p * blk, blk), blk)], qp_ref,
@@ -338,14 +345,14 @@
         c.wait()
 
 
-def tail_kernel(axis, n, o_ref, e1_hbm, g_hbm, m_ref, bg_ref, wout_ref, tin_ref, tout_ref, opm_ref,
+def tail_kernel(axis, n, heads, hd, scale, qsum_ref, cnt_ref, kv_ref, e1_hbm, g_hbm, m_ref, bg_ref, wout_ref, tin_ref, tout_ref, opm_ref,
                 z_hbm, ninv_ref, w_ref, bo_ref, e3_hbm, out_hbm,
-                e1_ref, g_ref, e3_ref, z_ref, buf_ref, a_ref, b_ref, ag_ref, tr_ref, bg_all, at_ref, hi_ref, lo_ref,
+                o_ref, l_ref, qp_ref, qb_ref, st_ref, sp_ref, csend, crecv, e1_ref, g_ref, e3_ref, z_ref, buf_ref, a_ref, b_ref, ag_ref, tr_ref, bg_all, at_ref, hi_ref, lo_ref,
                 wp_ref, wf_ref, local, asend, arecv, bsend, brecv):
     rows, res, pd = z_ref.shape
     nb, odim, ns, jb = b_ref.shape
     chips = a_ref.shape[0]
-    ht = o_ref.shape[0]
+    ht = heads * hd
     wide = e1_ref.shape[2]
     us = wide // res
     tb = buf_ref.shape[1]
@@ -400,12 +407,14 @@
 
     wout, tin, opm = (flip(r[...]) for r in (wout_ref, tin_ref, opm_ref))
     gate_bias = column(bg_ref[...])
+    column_attention(axis, n, heads, hd, scale, qsum_ref, cnt_ref, kv_ref, m_ref, o_ref,
+                     l_ref, qp_ref, qb_ref, st_ref, sp_ref, csend, crecv)
 
     def group(g, _):
         seqs = pl.ds(pl.multiple_of(g * tb, tb), tb)
         for c in fetch(g):
             c.wait()
-        o = jnp.concatenate([o_ref[...]] * us, axis=1)
+        o = jnp.concatenate([o_ref[...].reshape(ht, res)] * us, axis=1)
         for j in range(per):
             gr = g * per + j
             gated = (sigmoid(g_ref[gr].astype(F32) + gate_bias) * o).astype(BF16)
@@ -571,34 +580,24 @@
                        jax.ShapeDtypeStruct((ng, 2 * hd, wide), BF16), jax.ShapeDtypeStruct((ht, res), F32)],
             scratch_shapes=[pltpu.VMEM((us, 2 * ht + 16, heads * res), BF16), pltpu.VMEM((wide, 2 * ht + 16), BF16),
                             pltpu.VMEM((heads // 2, 32, wide), BF16), pltpu.VMEM((ht, wide), F32),
-                            pltpu.VMEM((heads // 2, res, 2 * res), F32), pltpu.VMEM((4 * ht, ch), BF16),
+                            pltpu.VMEM((heads // 2, res, 2 * res), F32), pltpu.VMEM((ch, wide), BF16), pltpu.VMEM((4 * ht, ch), BF16),
                             pltpu.VMEM((ch, ht), BF16), pltpu.VMEM((ncol, ch), BF16), pltpu.VMEM((ht, 1), F32), pltpu.SMEM((1,), F32)],
             compiler_params=params(dimension_semantics=('arbitrary',)),
             name='row_attention',
         )(jnp.transpose(msa, (0, 2, 1)), mask, packed, w_row_in, b_row_gate.reshape(1, ht), w_row_out, w_col_in)
 
-        col_o = pl.pallas_call(
-            functools.partial(col_kernel, 'seq', n_seq, heads, hd, scale),
-            in_specs=[pl.BlockSpec(memory_space=pltpu.VMEM)] * 4,
-            out_specs=pl.BlockSpec(memory_space=pltpu.VMEM),
-            out_shape=jax.ShapeDtypeStruct((heads, hd, res), F32),
-            scratch_shapes=[pltpu.VMEM((ng, heads, wide), F32), pltpu.VMEM((n_seq, ht // n_seq, res), F32),
-                            pltpu.VMEM((n_seq, ht // n_seq, res), F32), pltpu.VMEM((heads, 16, res), F32),
-                            pltpu.VMEM((n_seq, 16, res), F32), pltpu.SemaphoreType.DMA((4, n_seq)),
-                            pltpu.SemaphoreType.DMA((4, n_seq))],
-            compiler_params=params(collective_id=0, has_side_effects=True),
-            name='col_stats',
-        )(qsum, counts, kv, mask).reshape(ht, res)
-
         tb, jb, ib = 16, 128, 8
         chips = n_seq // 2
         nb = res // jb
         e3, pair_out = pl.pallas_call(
-            functools.partial(tail_kernel, 'seq', n_seq),
-            in_specs=[vm, hbm, hbm] + [vm] * 6 + [hbm] + [vm] * 3,
+            functools.partial(tail_kernel, 'seq', n_seq, heads, hd, scale),
+            in_specs=[vm] * 3 + [hbm] * 2 + [vm] * 6 + [hbm] + [vm] * 3,
             out_specs=[hbm, hbm],
             out_shape=[jax.ShapeDtypeStruct((ns, ch, res), BF16), jax.ShapeDtypeStruct((rows, res, pd), BF16)],
-            scratch_shapes=[pltpu.VMEM((ng, ch, wide), BF16), pltpu.VMEM((ng, ht, wide), BF16), pltpu.VMEM((ns, ch, res), BF16),
+            scratch_shapes=[pltpu.VMEM((heads, hd, res), F32), pltpu.VMEM((ng, heads, wide), F32),
+                            pltpu.VMEM((n_seq, ht // n_seq, res), F32), pltpu.VMEM((n_seq, ht // n_seq, res), F32),
+                            pltpu.VMEM((heads, 16, res), F32), pltpu.VMEM((n_seq, 16, res), F32), dma((4, n_seq)), dma((4, n_seq)),
+                            pltpu.VMEM((ng, ch, wide), BF16), pltpu.VMEM((ng, ht, wide), BF16), pltpu.VMEM((ns, ch, res), BF16),
                             pltpu.VMEM((rows, res, pd), BF16), pltpu.VMEM((2 * odim, tb, res), F32),
                             pltpu.VMEM((chips, odim, ns, jb), BF16), pltpu.VMEM((nb, odim, ns, jb), BF16),
                             pltpu.VMEM((n_seq, odim, ns, jb), BF16), pltpu.VMEM((2, odim // 2, ns, jb), BF16),
@@ -609,7 +608,7 @@
                             dma((ns // tb + nb - 1, 9)), dma((ns // tb + nb - 1, 9))],
             compiler_params=params(collective_id=2, has_side_effects=True),
             name='tail_outer_product',
-        )(col_o, e1, gate, mask, b_col_gate.reshape(1, ht), w_col_out, w_trans_in, w_trans_out.T, w_opm_in,
+        )(qsum, counts, kv, e1, gate, mask, b_col_gate.reshape(1, ht), w_col_out, w_trans_in, w_trans_out.T, w_opm_in,
           pair, ninv, w_opm_out, b_opm_out.reshape(1, pd))
         return jnp.transpose(e3, (0, 2, 1)), pair_out
 

time: 265 us -> 251 us (0.947)
  Pallas kernels: 258 us -> 244 us
    pallas_call x1, Pallas kernels: 107 us -> 98.1 us  [local_block(): pl.pallas_call(functools.partial(row_kernel, heads, hd, scale), grid=(ng,...]
    pallas_call x2 -> x1, Pallas kernels: 128 us -> 123 us  [local_block(): pl.pallas_call(functools.partial(tail_kernel, 'seq', n_seq, heads, hd, sc...]
where the time goes in v4:
time: 251 us
  Pallas kernels  244 us (97%)
  local copies, waits for them, and re-layouts  6.23 us (2%)
    pallas_call x1, Pallas kernels, local_block(): pl.pallas_call(functools.partial(tail_kernel, 'seq', n_seq, heads, hd, sc...  123 us
    pallas_call x1, Pallas kernels, local_block(): pl.pallas_call(functools.partial(row_kernel, heads, hd, scale), grid=(ng,...  98.1 us
    pallas_call x1, Pallas kernels, local_block(): pl.pallas_call(functools.partial(bias_kernel, 'seq', n_seq), in_specs=[hb...  23.2 us
    unnamed x4, local copies, waits for them, and re-layouts  6.23 us

profile of v4, /device:TPU:113, one launch (start us, length us, event | category | flops | bytes accessed | tf_op | source)
XLA Modules:
  0.0 251.3 jit_solution(8614180861327081116)
XLA Ops:
  0.6 23.2 %pair_bias.1 = (bf16[8,3,8,16,384]{4,3,2,1,0:T(8,128)(2,1)}, bf16[8,64,384]{2,1,0:T(8,128)(2,1)}, f32[48,1,384]{2,1,0:T(1,128)}, f32[1,384]{1,0:T(1,128)}) custom-call(bf16[48,384,128]{2,1,0:T(8,128)(2,1)} %z_hbm.3, bf16[8,128]{1,0:T(8,128)(2,1)} %bitcast.10, s32[64,384]{1,0:T(8,128)} %m_ref.5), custom_call_target="tpu_custom_call" | custom-call | tf_op jit(solution)/shard_map/pair_bias/pallas_call | solution.py:555
  23.9 98.1 %row_attention.1 = (bf16[8,64,3072]{2,1,0:T(8,128)(2,1)}, bf16[8,64,3072]{2,1,0:T(8,128)(2,1)}, bf16[8,16,3072]{2,1,0:T(8,128)(2,1)}, f32[64,384]{1,0:T(8,128)}) custom-call(bf16[64,64,384]{2,1,0:T(8,128)(2,1)} %bitcast.7, s32[64,384]{1,0:T(8,128)} %m_ref.5, bf16[8,3,8,16,384]{4,3,2,1,0:T(8,128)(2,1)} %get-tuple-element.11.packed_ref, ...), custom_call_target="tpu_custom_call" | custom-call | tf_op jit(solution)/shard_map/row_attention/pallas_call | solution.py:573
  121.9 123.1 %tail_outer_product.1 = (bf16[64,64,384]{2,1,0:T(8,128)(2,1)}, bf16[48,384,128]{2,1,0:T(8,128)(2,1)}) custom-call(f32[64,384]{1,0:T(8,128)} %get-tuple-element.12.qsum_ref, f32[1,384]{1,0:T(1,128)} %get-tuple-element.13.cnt_ref, bf16[8,16,3072]{2,1,0:T(8,128)(2,1)} %get-tuple-element.14.kv_ref, bf16[8,64,3072]{2,1,0:T(8,128)(2,1)} %get-tuple-element.15.e1_hbm, ...), custom_call_target="tpu_custom_call" | custom-call | tf_op jit(solution)/shard_map/tail_outer_product/pallas_call | solution.py:592
  245.0 0.0 copy-start
  245.0 4.0 %copy.19 = bf16[64,384,64]{1,2,0:T(8,128)(2,1)} copy(bf16[64,384,64]{1,2,0:T(8,128)(2,1)} %bitcast.8) | data formatting | bytes 6291456
  249.1 0.0 copy-done
  249.1 2.2 copy.20
Async XLA Ops:
  245.0 4.0 %copy-start = (bf16[48,384,128]{2,1,0:T(8,128)(2,1)S(1)}, bf16[48,384,128]{2,1,0:T(8,128)(2,1)}, u32[]{:S(2)}) copy-start(bf16[48,384,128]{2,1,0:T(8,128)(2,1)} %get-tuple-element.23) | copy-start | bytes 14155780

commit v5 on v4

--- a/solution.py
+++ b/solution.py
@@ -15,6 +15,7 @@
 VMEM_LIMIT = 62 * 1024 * 1024
 MESH = pl.DeviceIdType.MESH
 SEQS = 8
+GROUP = 4
 
 
 def norm_rows(x):
@@ -161,7 +162,7 @@
 
 def row_kernel(heads, hd, scale, e_ref, m_ref, packed_ref, win_ref, bg_ref, wout_ref, cin_ref,
                e1_ref, g_ref, kv_ref, qsum_ref,
-               rhs_ref, kaug_ref, va_ref, att_ref, bias_ref, xn_ref, wt_ref, ot_ref, ct_ref, gb_ref, top_ref):
+               rhs_ref, kaug_ref, v_ref, att_ref, bias_ref, xn_ref, wt_ref, ot_ref, ct_ref, gb_ref, top_ref):
     us, ch, res = e_ref.shape
     ht = heads * hd
     wide = us * res
@@ -170,7 +171,7 @@
     @pl.when(step == 0)
     def _():
         rows = lax.broadcasted_iota(jnp.int32, rhs_ref.shape, 1)
-        rhs_ref[...] = jnp.where(rows == 2 * ht, 1.0, 0.0).astype(BF16)
+        rhs_ref[...] = jnp.where(rows == 2 * GROUP * hd, 1.0, 0.0).astype(BF16)
         qsum_ref[...] = jnp.zeros_like(qsum_ref)
         wt_ref[...] = flip(win_ref[...])
         ot_ref[...] = flip(wout_ref[...])
@@ -182,10 +183,10 @@
         for h in range(heads):
             one = jnp.concatenate([packed_ref[d, t, h] for d in range(packed_ref.shape[0])
                                    for t in range(packed_ref.shape[1])], axis=0)
-            bias_ref[h // 2, :, (h % 2) * res:(h % 2 + 1) * res] = jnp.transpose(one.astype(F32)) * LOG2E
+            bias_ref[h // GROUP, :, (h % GROUP) * res:(h % GROUP + 1) * res] = jnp.transpose(one.astype(F32)) * LOG2E
         top = jnp.abs(bias_ref[0])
-        for pr in range(1, heads // 2):
-            top = jnp.maximum(top, jnp.abs(bias_ref[pr]))
+        for gr in range(1, heads // GROUP):
+            top = jnp.maximum(top, jnp.abs(bias_ref[gr]))
         top_ref[0] = wide_max(top)
 
     def source():
@@ -205,32 +206,38 @@
     k_top = wide_max(dot(per_head, k * k))
     small = (q_top * k_top < 880.0) & (top_ref[0] < 30.0) & (wide_max(jnp.abs(v)) < 1e15)
 
-    first_half = (lax.broadcasted_iota(jnp.int32, (ht, wide), 0) % 16) < 8
+    gw = GROUP * hd
+    row_head = (lax.broadcasted_iota(jnp.int32, (ht, wide), 0) // hd) % GROUP
     hi = qs.astype(BF16).astype(F32)
     for n, part in enumerate((hi, qs - hi)):
-        even = jnp.where(first_half, part, 0.0).astype(BF16)
-        odd = jnp.where(first_half, 0.0, part).astype(BF16)
-        for u in range(us):
-            for h in range(heads):
-                rows = slice(16 * (h // 2), 16 * (h // 2) + 16)
-                rhs_ref[u, n * ht + rows.start:n * ht + rows.stop, h * res:(h + 1) * res] = \
-                    (odd if h % 2 else even)[rows, u * res:(u + 1) * res]
+        for r in range(GROUP):
+            only = jnp.where(row_head == r, part, 0.0).astype(BF16)
+            for u in range(us):
+                for h in range(r, heads, GROUP):
+                    rhs_ref[u, gw * n:gw * (n + 1), h * res:(h + 1) * res] = \
+                        only[gw * (h // GROUP):gw * (h // GROUP + 1), u * res:(u + 1) * res]
     pen = jnp.where(lax.broadcasted_iota(jnp.int32, (16, wide), 0) == 0,
                     jnp.broadcast_to(jnp.where(keep > 0, 0.0, -1e30), (16, wide)), 0.0)
-    kaug_ref[...] = jnp.transpose(jnp.concatenate([k, k, pen.astype(BF16)], axis=0))
-    ones = jnp.where(lax.broadcasted_iota(jnp.int32, (8, wide), 0) == 0, 1.0, 0.0)
-    for pr in range(heads // 2):
-        va_ref[pr] = jnp.concatenate([v[16 * pr:16 * pr + 8], ones, v[16 * pr + 8:16 * pr + 16], ones], axis=0).astype(BF16)
+    for gr in range(heads // GROUP):
+        kp = k[gw * gr:gw * (gr + 1)]
+        kaug_ref[gr] = jnp.transpose(jnp.concatenate([kp, kp, pen.astype(BF16)], axis=0))
+    v_ref[...] = v.astype(BF16)
+
+    def attend(cols, gr, rows, lanes, at_row, shifted):
+        s = dot(kaug_ref[gr, cols], lanes) + bias_ref[gr]
+        p = jnp.exp2(s - jnp.max(s, axis=0, keepdims=True)) if shifted else jnp.exp2(s)
+        den = jnp.sum(p, axis=0, keepdims=True)
+        o = dot(v_ref[rows, cols], p.astype(BF16))
+        for r in range(GROUP):
+            att_ref[at_row(r), cols] = o[hd * r:hd * (r + 1), r * res:(r + 1) * res] / den[:, r * res:(r + 1) * res]
 
     @pl.when(small)
     def _():
         for u in range(us):
             cols = slice(u * res, (u + 1) * res)
-            for pr in range(heads // 2):
-                s = dot(kaug_ref[cols], rhs_ref[u, :, 2 * pr * res:(2 * pr + 2) * res]) + bias_ref[pr]
-                o = dot(va_ref[pr, :, cols], jnp.exp2(s).astype(BF16))
-                att_ref[16 * pr:16 * pr + 8, cols] = o[0:8, :res] / o[8:9, :res]
-                att_ref[16 * pr + 8:16 * pr + 16, cols] = o[16:24, res:] / o[24:25, res:]
+            for gr in range(heads // GROUP):
+                attend(cols, gr, slice(gw * gr, gw * (gr + 1)), rhs_ref[u, :, gr * GROUP * res:(gr + 1) * GROUP * res],
+                       lambda r: slice(gw * gr + hd * r, gw * gr + hd * (r + 1)), False)
             some = jnp.max(keep[:, cols], axis=1, keepdims=True) > 0
             flat = jnp.mean(v[:, cols], axis=1, keepdims=True)
             att_ref[:, cols] = jnp.where(some, att_ref[:, cols], flat)
@@ -238,16 +245,14 @@
     @pl.when(jnp.logical_not(small))
     def _():
         def one(t, _):
-            u, pr = t // (heads // 2), t % (heads // 2)
+            u, gr = t // (heads // GROUP), t % (heads // GROUP)
             cols = pl.ds(pl.multiple_of(u * res, res), res)
-            s = dot(kaug_ref[cols], rhs_ref[u, :, pl.ds(pl.multiple_of(2 * pr * res, 2 * res), 2 * res)]) + bias_ref[pr]
-            p = jnp.exp2(s - jnp.max(s, axis=0, keepdims=True)).astype(BF16)
-            o = dot(va_ref[pr, :, cols], p)
-            att_ref[pl.ds(pl.multiple_of(16 * pr, 16), 8), cols] = o[0:8, :res] / o[8:9, :res]
-            att_ref[pl.ds(pl.multiple_of(16 * pr + 8, 8), 8), cols] = o[16:24, res:] / o[24:25, res:]
+            attend(cols, gr, pl.ds(pl.multiple_of(gw * gr, gw), gw),
+                   rhs_ref[u, :, pl.ds(pl.multiple_of(gr * GROUP * res, GROUP * res), GROUP * res)],
+                   lambda r: pl.ds(pl.multiple_of(gw * gr + hd * r, hd), hd), True)
             return 0
 
-        lax.fori_loop(0, us * (heads // 2), one, 0)
+        lax.fori_loop(0, us * (heads // GROUP), one, 0)
 
     gated = (sigmoid(project(3).astype(F32) + gb_ref[...]) * att_ref[...]).astype(BF16)
     e1 = (source() + dot(ot_ref[...], gated)).astype(BF16)
@@ -578,9 +583,9 @@
             out_specs=[group(1, ch), group(1, ht), group(1, 2 * hd), full(ht, res)],
             out_shape=[jax.ShapeDtypeStruct((ng, ch, wide), BF16), jax.ShapeDtypeStruct((ng, ht, wide), BF16),
                        jax.ShapeDtypeStruct((ng, 2 * hd, wide), BF16), jax.ShapeDtypeStruct((ht, res), F32)],
-            scratch_shapes=[pltpu.VMEM((us, 2 * ht + 16, heads * res), BF16), pltpu.VMEM((wide, 2 * ht + 16), BF16),
-                            pltpu.VMEM((heads // 2, 32, wide), BF16), pltpu.VMEM((ht, wide), F32),
-                            pltpu.VMEM((heads // 2, res, 2 * res), F32), pltpu.VMEM((ch, wide), BF16), pltpu.VMEM((4 * ht, ch), BF16),
+            scratch_shapes=[pltpu.VMEM((us, 2 * GROUP * hd + 16, heads * res), BF16), pltpu.VMEM((heads // GROUP, wide, 2 * GROUP * hd + 16), BF16),
+                            pltpu.VMEM((ht, wide), BF16), pltpu.VMEM((ht, wide), F32),
+                            pltpu.VMEM((heads // GROUP, res, GROUP * res), F32), pltpu.VMEM((ch, wide), BF16), pltpu.VMEM((4 * ht, ch), BF16),
                             pltpu.VMEM((ch, ht), BF16), pltpu.VMEM((ncol, ch), BF16), pltpu.VMEM((ht, 1), F32), pltpu.SMEM((1,), F32)],
             compiler_params=params(dimension_semantics=('arbitrary',)),
             name='row_attention',

time: 251 us -> 242 us (0.964)
  Pallas kernels: 244 us -> 235 us
    pallas_call x1, Pallas kernels: 98.1 us -> 88 us  [local_block(): pl.pallas_call(functools.partial(row_kernel, heads, hd, scale), grid=(ng,...]
where the time goes in v5:
time: 242 us; the launch traced here: 241 us
  Pallas kernels  235 us (97%)
  local copies, waits for them, and re-layouts  6.23 us (3%)
    pallas_call x1, Pallas kernels, local_block(): pl.pallas_call(functools.partial(tail_kernel, 'seq', n_seq, heads, hd, sc...  123 us
    pallas_call x1, Pallas kernels, local_block(): pl.pallas_call(functools.partial(row_kernel, heads, hd, scale), grid=(ng,...  88 us
    pallas_call x1, Pallas kernels, local_block(): pl.pallas_call(functools.partial(bias_kernel, 'seq', n_seq), in_specs=[hb...  23.2 us
    unnamed x4, local copies, waits for them, and re-layouts  6.23 us

profile of v5, /device:TPU:113, one launch (start us, length us, event | category | flops | bytes accessed | tf_op | source)
XLA Modules:
  0.0 241.5 jit_solution(10214134638628437739)
XLA Ops:
  0.6 23.2 %pair_bias.1 = (bf16[8,3,8,16,384]{4,3,2,1,0:T(8,128)(2,1)}, bf16[8,64,384]{2,1,0:T(8,128)(2,1)}, f32[48,1,384]{2,1,0:T(1,128)}, f32[1,384]{1,0:T(1,128)}) custom-call(bf16[48,384,128]{2,1,0:T(8,128)(2,1)} %z_hbm.3, bf16[8,128]{1,0:T(8,128)(2,1)} %bitcast.10, s32[64,384]{1,0:T(8,128)} %m_ref.5), custom_call_target="tpu_custom_call" | custom-call | tf_op jit(solution)/shard_map/pair_bias/pallas_call | solution.py:560
  23.9 88.0 %row_attention.1 = (bf16[8,64,3072]{2,1,0:T(8,128)(2,1)}, bf16[8,64,3072]{2,1,0:T(8,128)(2,1)}, bf16[8,16,3072]{2,1,0:T(8,128)(2,1)}, f32[64,384]{1,0:T(8,128)}) custom-call(bf16[64,64,384]{2,1,0:T(8,128)(2,1)} %bitcast.7, s32[64,384]{1,0:T(8,128)} %m_ref.5, bf16[8,3,8,16,384]{4,3,2,1,0:T(8,128)(2,1)} %get-tuple-element.11.packed_ref, ...), custom_call_target="tpu_custom_call" | custom-call | tf_op jit(solution)/shard_map/row_attention/pallas_call | solution.py:578
  111.9 123.3 %tail_outer_product.1 = (bf16[64,64,384]{2,1,0:T(8,128)(2,1)}, bf16[48,384,128]{2,1,0:T(8,128)(2,1)}) custom-call(f32[64,384]{1,0:T(8,128)} %get-tuple-element.12.qsum_ref, f32[1,384]{1,0:T(1,128)} %get-tuple-element.13.cnt_ref, bf16[8,16,3072]{2,1,0:T(8,128)(2,1)} %get-tuple-element.14.kv_ref, bf16[8,64,3072]{2,1,0:T(8,128)(2,1)} %get-tuple-element.15.e1_hbm, ...), custom_call_target="tpu_custom_call" | custom-call | tf_op jit(solution)/shard_map/tail_outer_product/pallas_call | solution.py:597
  235.2 0.0 copy-start
  235.2 4.0 %copy.19 = bf16[64,384,64]{1,2,0:T(8,128)(2,1)} copy(bf16[64,384,64]{1,2,0:T(8,128)(2,1)} %bitcast.8) | data formatting | bytes 6291456
  239.3 0.0 copy-done
  239.3 2.2 copy.20
Async XLA Ops:
  235.2 4.0 %copy-start = (bf16[48,384,128]{2,1,0:T(8,128)(2,1)S(1)}, bf16[48,384,128]{2,1,0:T(8,128)(2,1)}, u32[]{:S(2)}) copy-start(bf16[48,384,128]{2,1,0:T(8,128)(2,1)} %get-tuple-element.23) | copy-start | bytes 14155780

commit v6 on v5

--- a/solution.py
+++ b/solution.py
@@ -33,7 +33,7 @@
 
 
 def sigmoid(x):
-    return 1.0 / (1.0 + jnp.exp(-x))
+    return 0.5 * jnp.tanh(0.5 * x) + 0.5
 
 
 def wide_max(x):
@@ -226,8 +226,8 @@
     def attend(cols, gr, rows, lanes, at_row, shifted):
         s = dot(kaug_ref[gr, cols], lanes) + bias_ref[gr]
         p = jnp.exp2(s - jnp.max(s, axis=0, keepdims=True)) if shifted else jnp.exp2(s)
-        den = jnp.sum(p, axis=0, keepdims=True)
-        o = dot(v_ref[rows, cols], p.astype(BF16))
+        o = dot(jnp.concatenate([v_ref[rows, cols], jnp.ones((16, res), BF16)], axis=0), p.astype(BF16))
+        den = o[gw:gw + 1]
         for r in range(GROUP):
             att_ref[at_row(r), cols] = o[hd * r:hd * (r + 1), r * res:(r + 1) * res] / den[:, r * res:(r + 1) * res]
 
@@ -353,7 +353,7 @@
 def tail_kernel(axis, n, heads, hd, scale, qsum_ref, cnt_ref, kv_ref, e1_hbm, g_hbm, m_ref, bg_ref, wout_ref, tin_ref, tout_ref, opm_ref,
                 z_hbm, ninv_ref, w_ref, bo_ref, e3_hbm, out_hbm,
                 o_ref, l_ref, qp_ref, qb_ref, st_ref, sp_ref, csend, crecv, e1_ref, g_ref, e3_ref, z_ref, buf_ref, a_ref, b_ref, ag_ref, tr_ref, bg_all, at_ref, hi_ref, lo_ref,
-                wp_ref, wf_ref, local, asend, arecv, bsend, brecv):
+                wp_ref, wf_ref, place_ref, local, asend, arecv, bsend, brecv):
     rows, res, pd = z_ref.shape
     nb, odim, ns, jb = b_ref.shape
     chips = a_ref.shape[0]
@@ -383,11 +383,13 @@
     enter(axis, me, n)
 
     part = {None: slice(None), 0: pl.ds(0, half), 1: pl.ds(half, half)}
+    quad = a_ref.shape[1]
+    apart = {None: slice(None), 0: pl.ds(0, quad // 2), 1: pl.ds(quad // 2, quad // 2)}
 
     def a_copies(g):
         seqs = pl.ds(pl.multiple_of(g * tb, tb), tb)
-        src = lambda c, p=None: a_ref.at[c, part[p], seqs]
-        dst = lambda d, p=None: ag_ref.at[d, part[p], seqs]
+        src = lambda c, p=None: a_ref.at[c, apart[p], seqs]
+        dst = lambda d, p=None: ag_ref.at[d, apart[p], seqs]
         tr = lambda t: tr_ref.at[t, :, seqs]
         plan = [(src(across, 0), tr(0), right), (src(across, 1), tr(1), left), (src(up), dst(me), right),
                 (src(down), dst(me), left), (src(chip), dst(me), other),
@@ -405,10 +407,13 @@
         return Gather(axis, me, n, lambda k: (bsend.at[ngr - 1 + t, k], brecv.at[ngr - 1 + t, k]), b_ref.at[t],
                       lambda d, p=None: bg_all.at[t, d] if p is None else bg_all.at[t, d, part[p]])
 
-    src = lax.broadcasted_iota(jnp.int32, (res, chips * jb), 0)
-    dst = lax.broadcasted_iota(jnp.int32, (res, chips * jb), 1)
-    hj = jb // 2
-    place = ((dst % hj < rows) & (src == (dst // hj) * rows + dst % hj)).astype(BF16)
+    pack = odim // quad
+    src = lax.broadcasted_iota(jnp.int32, (res, chips * res), 0)
+    dst = lax.broadcasted_iota(jnp.int32, (res, chips * res), 1)
+    for r in range(pack):
+        where = (dst // res) * (2 * rows) + dst % res - r * 2 * rows
+        ok = (dst % res >= r * 2 * rows) & (dst % res < (r + 1) * 2 * rows)
+        place_ref[r] = (ok & (src == where)).astype(BF16)
 
     wout, tin, opm = (flip(r[...]) for r in (wout_ref, tin_ref, opm_ref))
     gate_bias = column(bg_ref[...])
@@ -431,9 +436,9 @@
                 cols = slice(u * res, (u + 1) * res)
                 e3_ref[gr * us + u] = e3[:, cols]
                 buf_ref[:, j * us + u, :] = ab[:, cols]
-        moved = dot(buf_ref[0:odim].astype(BF16).reshape(odim * tb, res), place).astype(BF16)
+        moved = sum(dot(buf_ref[r * quad:(r + 1) * quad].astype(BF16).reshape(quad * tb, res), place_ref[r]) for r in range(pack))
         for c in range(chips):
-            a_ref[c, :, seqs, :] = moved[:, c * jb:(c + 1) * jb].reshape(odim, tb, jb)
+            a_ref[c, :, seqs, :] = moved[:, c * res:(c + 1) * res].astype(BF16).reshape(quad, tb, res)
         for t in range(nb):
             blk = buf_ref[odim:, :, t * jb:(t + 1) * jb].astype(BF16)
             b_ref[t, :, seqs, :] = blk
@@ -475,10 +480,13 @@
     wf_ref[...] = w_ref[...].astype(F32)
     for d in range(odim):
         wp_ref[:, d * odim:(d + 1) * odim] = jnp.transpose(wf_ref[:, d, :]).astype(BF16)
-    pick = (lax.broadcasted_iota(jnp.int32, (rows, jb), 1) ==
-            lax.broadcasted_iota(jnp.int32, (rows, jb), 0) + core * hj).astype(BF16)
-    for c in range(odim):
-        at_ref[:, c, :] = dot_t(pick, ag_ref[:, c].reshape(n * ns, jb))
+    row = lax.broadcasted_iota(jnp.int32, (pack * rows, res), 0)
+    pick = (lax.broadcasted_iota(jnp.int32, (pack * rows, res), 1) ==
+            (row // rows) * (2 * rows) + row % rows + core * rows).astype(BF16)
+    for q in range(quad):
+        got = dot_t(pick, ag_ref[:, q].reshape(n * ns, res))
+        for r in range(pack):
+            at_ref[:, r * quad + q, :] = got[r * rows:(r + 1) * rows]
 
     def finish_b(g, _):
         b_first(g).close()
@@ -594,6 +602,7 @@
         tb, jb, ib = 16, 128, 8
         chips = n_seq // 2
         nb = res // jb
+        quad = odim * 2 * rows // res
         e3, pair_out = pl.pallas_call(
             functools.partial(tail_kernel, 'seq', n_seq, heads, hd, scale),
             in_specs=[vm] * 3 + [hbm] * 2 + [vm] * 6 + [hbm] + [vm] * 3,
@@ -604,11 +613,12 @@
                             pltpu.VMEM((heads, 16, res), F32), pltpu.VMEM((n_seq, 16, res), F32), dma((4, n_seq)), dma((4, n_seq)),
                             pltpu.VMEM((ng, ch, wide), BF16), pltpu.VMEM((ng, ht, wide), BF16), pltpu.VMEM((ns, ch, res), BF16),
                             pltpu.VMEM((rows, res, pd), BF16), pltpu.VMEM((2 * odim, tb, res), F32),
-                            pltpu.VMEM((chips, odim, ns, jb), BF16), pltpu.VMEM((nb, odim, ns, jb), BF16),
-                            pltpu.VMEM((n_seq, odim, ns, jb), BF16), pltpu.VMEM((2, odim // 2, ns, jb), BF16),
+                            pltpu.VMEM((chips, quad, ns, res), BF16), pltpu.VMEM((nb, odim, ns, jb), BF16),
+                            pltpu.VMEM((n_seq, quad, ns, res), BF16), pltpu.VMEM((2, quad // 2, ns, res), BF16),
                             pltpu.VMEM((nb, n_seq, odim, ns, jb), BF16), pltpu.VMEM((rows, odim, n_seq * ns), F32),
                             pltpu.VMEM((ib // 2, odim * odim, 2 * jb), BF16), pltpu.VMEM((ib // 2, odim * odim, 2 * jb), BF16),
                             pltpu.VMEM((pd, odim * odim), BF16), pltpu.VMEM((odim, odim, pd), F32),
+                            pltpu.VMEM((odim // quad, res, chips * res), BF16),
                             dma((4, max(4, ns // tb))), dma((ns // tb, 11)), dma((ns // tb, 11)),
                             dma((ns // tb + nb - 1, 9)), dma((ns // tb + nb - 1, 9))],
             compiler_params=params(collective_id=2, has_side_effects=True),

time: 242 us -> 238 us (0.983)
  Pallas kernels: 235 us -> 231 us
    pallas_call x1, Pallas kernels: 123 us -> 120 us  [local_block(): pl.pallas_call(functools.partial(tail_kernel, 'seq', n_seq, heads, hd, sc...]
where the time goes in v6:
time: 238 us
  Pallas kernels  231 us (97%)
  local copies, waits for them, and re-layouts  6.23 us (3%)
    pallas_call x1, Pallas kernels, local_block(): pl.pallas_call(functools.partial(tail_kernel, 'seq', n_seq, heads, hd, sc...  120 us
    pallas_call x1, Pallas kernels, local_block(): pl.pallas_call(functools.partial(row_kernel, heads, hd, scale), grid=(ng,...  87.4 us
    pallas_call x1, Pallas kernels, local_block(): pl.pallas_call(functools.partial(bias_kernel, 'seq', n_seq), in_specs=[hb...  23.2 us
    unnamed x4, local copies, waits for them, and re-layouts  6.23 us

profile of v6, /device:TPU:113, one launch (start us, length us, event | category | flops | bytes accessed | tf_op | source)
XLA Modules:
  0.0 238.0 jit_solution(12910629611646112269)
XLA Ops:
  0.6 23.2 %pair_bias.1 = (bf16[8,3,8,16,384]{4,3,2,1,0:T(8,128)(2,1)}, bf16[8,64,384]{2,1,0:T(8,128)(2,1)}, f32[48,1,384]{2,1,0:T(1,128)}, f32[1,384]{1,0:T(1,128)}) custom-call(bf16[48,384,128]{2,1,0:T(8,128)(2,1)} %z_hbm.3, bf16[8,128]{1,0:T(8,128)(2,1)} %bitcast.10, s32[64,384]{1,0:T(8,128)} %m_ref.5), custom_call_target="tpu_custom_call" | custom-call | tf_op jit(solution)/shard_map/pair_bias/pallas_call | solution.py:568
  23.9 87.4 %row_attention.1 = (bf16[8,64,3072]{2,1,0:T(8,128)(2,1)}, bf16[8,64,3072]{2,1,0:T(8,128)(2,1)}, bf16[8,16,3072]{2,1,0:T(8,128)(2,1)}, f32[64,384]{1,0:T(8,128)}) custom-call(bf16[64,64,384]{2,1,0:T(8,128)(2,1)} %bitcast.7, s32[64,384]{1,0:T(8,128)} %m_ref.5, bf16[8,3,8,16,384]{4,3,2,1,0:T(8,128)(2,1)} %get-tuple-element.11.packed_ref, ...), custom_call_target="tpu_custom_call" | custom-call | tf_op jit(solution)/shard_map/row_attention/pallas_call | solution.py:586
  111.3 120.4 %tail_outer_product.1 = (bf16[64,64,384]{2,1,0:T(8,128)(2,1)}, bf16[48,384,128]{2,1,0:T(8,128)(2,1)}) custom-call(f32[64,384]{1,0:T(8,128)} %get-tuple-element.12.qsum_ref, f32[1,384]{1,0:T(1,128)} %get-tuple-element.13.cnt_ref, bf16[8,16,3072]{2,1,0:T(8,128)(2,1)} %get-tuple-element.14.kv_ref, bf16[8,64,3072]{2,1,0:T(8,128)(2,1)} %get-tuple-element.15.e1_hbm, ...), custom_call_target="tpu_custom_call" | custom-call | tf_op jit(solution)/shard_map/tail_outer_product/pallas_call | solution.py:606
  231.8 0.0 copy-start
  231.8 4.0 %copy.19 = bf16[64,384,64]{1,2,0:T(8,128)(2,1)} copy(bf16[64,384,64]{1,2,0:T(8,128)(2,1)} %bitcast.8) | data formatting | bytes 6291456
  235.8 0.0 copy-done
  235.8 2.2 copy.20
Async XLA Ops:
  231.8 4.0 %copy-start = (bf16[48,384,128]{2,1,0:T(8,128)(2,1)S(1)}, bf16[48,384,128]{2,1,0:T(8,128)(2,1)}, u32[]{:S(2)}) copy-start(bf16[48,384,128]{2,1,0:T(8,128)(2,1)} %get-tuple-element.23) | copy-start | bytes 14155780
